TPU v7x, 256 devices: a whole 4x4x8 slice. The times are simulated.
256 devices in a mesh: field: 32 (over z, x), vrow: 2 (over core), vcol: 4 (over y).
Axes of the slice: x: 4, y: 4, z: 8, core: 2. Of those that a mesh axis runs over, the one named last changes fastest.
Arguments:
- blocks: bfloat16 [1024, 192, 2, 256], P(('vrow', 'vcol'), 'field'), may hold values from 0 to 1
- block_ids: int32 [8, 32, 6], P(('vrow', 'vcol'), 'field'), may hold values from 0 to 11, as said below
- block_counts: int32 [8, 32], P(('vrow', 'vcol'), 'field'), may hold values from 1 to 6, as said below
Outputs:
- tables: float32 [1024, 2, 2, 4, 2, 128], P(('vrow', 'field'), None, None, 'vcol')
Inputs may be any that keep to these rules, and one draw needn't show every extreme that they name: `block_ids`: within each row of the last dimension the entries are distinct. `block_counts`: 6 is reached in every draw.
All inputs are finite; a program needn't handle non-finite values.
Results may differ from a plain program's by a relative error of at most 0.0003.
Values may be sent and summed in bfloat16 or wider, within the bound.
No kernel may reach another device: no remote copies, remote signals or barrier semaphores. Data moves between devices by JAX's collectives and lax.ppermute only.
A program may use at most 64 MiB of HBM per device.

v0:
```python
import functools

import jax
import jax.numpy as jnp
from jax import lax
from jax.experimental import pallas as pl
from jax.experimental.pallas import tpu as pltpu
from jax.sharding import Mesh, PartitionSpec as P


SBLK = 12
OCC = 6
HALF = OCC // 2
BLOCK = 256
VS = 128
ROWS = HALF * 2 * VS
PARTS = [pl.ds(v, 16) for v in range(0, VS, 16)]
NX = 4
NSAMP = 98304

STEPS = 2730.0
TOP = 32767.0
BIAS = 32768.0


VM = pl.BlockSpec(memory_space=pltpu.VMEM)


def on_chip(f, out_shape, arrays, scratch, flops, aliases={}):
    arrays = [pltpu.with_memory_space_constraint(a, pltpu.VMEM) for a in arrays]
    many = isinstance(out_shape, tuple)
    return pl.pallas_call(
        f,
        out_shape=out_shape,
        in_specs=[VM] * len(arrays),
        out_specs=(VM,) * len(out_shape) if many else VM,
        scratch_shapes=scratch,
        input_output_aliases=aliases,
        cost_estimate=pl.CostEstimate(flops=flops, transcendentals=0, bytes_accessed=0),
        compiler_params=pltpu.CompilerParams(vmem_limit_bytes=12 << 20),
    )(*arrays)


def rotate(array, axis, shift):
    n = lax.axis_size(axis)
    return lax.ppermute(array, axis, [(i, (i + shift) % n) for i in range(n)])


def exponent(largest):
    return jnp.clip(jnp.ceil(jnp.log2(largest)), -100.0, 100.0)


def coded(values, exp):
    q = jnp.round((exp - jnp.log2(values)) * STEPS) - BIAS
    q = jnp.clip(q, -BIAS, TOP)
    return q.astype(jnp.int32).astype(jnp.int16)


def decoded(codes, exp):
    q = codes.astype(jnp.int32).astype(jnp.float32)
    return jnp.where(q >= TOP, 0.0, jnp.exp2((exp - BIAS / STEPS) - q * (1.0 / STEPS)))


def relay_kernel(blocks, a, b, held, sems):
    copies = [
        pltpu.make_async_copy(blocks.at[part], held.at[part], sems.at[i])
        for i, part in enumerate(PARTS)
    ]
    for copy in copies:
        copy.start()
    for part, copy in zip(PARTS, copies):
        copy.wait()
        for o in range(OCC):
            both = jnp.swapaxes(held[part, o], 0, 1)
            for c in range(2):
                to = (o % HALF) * 2 * VS + c * VS + part.start
                (a, b)[o // HALF][to : to + part.size, :] = both[c]


def relaid(blocks):
    half = pltpu.VMEM((ROWS, BLOCK), jnp.bfloat16)
    return pl.pallas_call(
        relay_kernel,
        out_shape=(half,) * 2,
        in_specs=[pl.BlockSpec(memory_space=pltpu.HBM)],
        out_specs=(VM,) * 2,
        scratch_shapes=[
            pltpu.VMEM(blocks.shape, jnp.bfloat16),
            pltpu.SemaphoreType.DMA((len(PARTS),)),
        ],
        compiler_params=pltpu.CompilerParams(vmem_limit_bytes=12 << 20),
    )(pltpu.with_memory_space_constraint(blocks, pltpu.HBM))


def tag_kernel(ids, count, a, b, tagged_a, tagged_b, tags):
    lane = lax.broadcasted_iota(jnp.int32, (16, BLOCK), 1)
    word = jnp.full((16, BLOCK), SBLK, jnp.int32)
    for o in range(OCC):
        word = jnp.where((lane == o) & (o < count[0]), ids[o], word)
    word = word.astype(jnp.float32).astype(jnp.bfloat16)
    tags[...] = word
    for half, out in ((a, tagged_a), (b, tagged_b)):
        out[:ROWS] = half[...]
        out[ROWS:] = word


def tagged(ids, count, halves):
    more = pltpu.VMEM((ROWS + 16, BLOCK), jnp.bfloat16)
    smem = pl.BlockSpec(memory_space=pltpu.SMEM)
    return pl.pallas_call(
        tag_kernel,
        out_shape=(more, more, pltpu.VMEM((16, BLOCK), jnp.bfloat16)),
        in_specs=[smem, smem, VM, VM],
        out_specs=(VM,) * 3,
        cost_estimate=pl.CostEstimate(flops=2 * 256**3, transcendentals=0, bytes_accessed=0),
        compiler_params=pltpu.CompilerParams(vmem_limit_bytes=12 << 20),
    )(ids, count, *(pltpu.with_memory_space_constraint(h, pltpu.VMEM) for h in halves))


def ids_of(ref):
    at = ref.shape[0] - 16
    tags = ref[at : at + 16, :VS].astype(jnp.float32)[:1]
    lane = lax.broadcasted_iota(jnp.int32, (1, VS), 1)
    weight = jnp.zeros((1, VS), jnp.float32)
    for o in range(OCC):
        weight = jnp.where(lane == o, float(16**o), weight)
    word = jnp.sum(tags * weight).astype(jnp.int32)
    return [(word >> (4 * o)) & 15 for o in range(OCC)]


def table_kernel(n, gathers, *refs):
    col_tags, row_tags, refs = refs[:2], refs[2 : 2 + n], refs[2 + n :]
    if gathers:
        (a0, b0, a1, b1), refs = refs[:4], refs[4:]
        rows = (a0, b0)
    else:
        cols, rows, refs = refs[0], refs[1 : 1 + 2 * n], refs[1 + 2 * n :]
    outs, refs = refs[:NX], refs[NX:]
    if gathers:
        cols, refs = refs[0], refs[1:]
        for s, halves in enumerate(((a0, b0), (a1, b1))):
            for o in range(OCC):
                cols[s, o] = halves[o // HALF][pl.ds((o % HALF) * 256, 256), :]
    slot_of, acc = refs
    x, core = lax.axis_index("x"), lax.axis_index("vrow")
    for s, ref in enumerate(col_tags):
        ids = ids_of(ref)
        for k in range(SBLK + 1):
            slot_of[s, k] = -1
        for o in range(OCC):
            slot_of[s, ids[o]] = o
        slot_of[s, SBLK] = -1
    row_ids = [ids_of(ref) for ref in row_tags]
    for j in range(n):
        largest = None
        for s in range(2):
            total = None
            for o in range(OCC):
                slot = slot_of[s, row_ids[j][o]]
                m = rows[2 * j + o // HALF][pl.ds((o % HALF) * 256, 256), :]
                m = jnp.where(slot >= 0, m, jnp.zeros_like(m))
                d = lax.dot_general(
                    m,
                    cols[s, jnp.maximum(slot, 0)],
                    (((1,), (1,)), ((), ())),
                    preferred_element_type=jnp.float32,
                )
                total = d if total is None else total + d
            acc[s] = total
            top = jnp.max(total)
            largest = top if largest is None else jnp.maximum(largest, top)
        exp = exponent(jnp.full((16, VS), largest, jnp.float32))
        for k in range(1, NX):
            outs[k][j, 256:272, :] = exp.astype(jnp.int32).astype(jnp.int16)
        for s in range(2):
            r = core if s == 0 else 1 - core
            for k in range(NX):
                there = lax.rem(x + k, NX) * 16
                for zz in range(2):
                    for a in range(2):
                        at = pl.ds(pl.multiple_of(there + a * VS + zz * 64, 16), 16)
                        for b in range(2):
                            v = acc[s, at, pl.ds(b * VS, VS)]
                            to = pl.multiple_of(r * 128 + (b * 64 + (zz * 2 + a) * 16), 16)
                            if k:
                                v = coded(v, exp)
                            outs[k][j, pl.ds(to, 16), :] = v


def tables(col_tags, row_tags, arrays, gathers=False):
    n = len(row_tags)
    kept = pltpu.VMEM((n, 256, VS), jnp.float32)
    sent = pltpu.VMEM((n, 272, VS), jnp.int16)
    outs = (kept,) + (sent,) * (NX - 1)
    if gathers:
        outs += (pltpu.VMEM((2, OCC, 2 * VS, BLOCK), jnp.bfloat16),)
    return on_chip(
        functools.partial(table_kernel, n, gathers),
        outs,
        [*col_tags, *row_tags, *arrays],
        [pltpu.SMEM((2, 16), jnp.int32), pltpu.VMEM((2, 256, 256), jnp.float32)],
        n * 12 * 2 * 256**3,
    )


def sum_kernel(n, shifts, *refs):
    ins, (out, acc) = refs[: n * NX], refs[-2:]
    y = lax.axis_index("vcol")
    for g, group in enumerate(shifts):
        mine = ins[g * NX : g * NX + NX]
        for j, shift in enumerate(group):
            p = lax.rem(y + shift, 4)
            exps = [mine[k][j, 256:272, :].astype(jnp.int32).astype(jnp.float32)[:1] for k in range(1, NX)]
            largest = None
            for rb in range(4):
                part = pl.ds(rb * 64, 64)
                total = mine[0][j, part, :]
                for k in range(1, NX):
                    total = total + decoded(mine[k][j, part, :], exps[k - 1])
                acc[part, :] = total
                largest = total if largest is None else jnp.maximum(largest, total)
            exp = exponent(jnp.full((16, VS), jnp.max(largest), jnp.float32))
            for zz in range(2):
                to = 2 * p + zz
                out[to, 128:144, :] = exp.astype(jnp.int32).astype(jnp.int16)
                for rb in range(4):
                    v = acc[pl.ds(rb * 64 + zz * 32, 32), :]
                    out[to, rb * 32 : rb * 32 + 32, :] = coded(v, exp[:1])


def summed(shifts, pieces, base=None):
    n = len(shifts)
    extra = [] if base is None else [base]
    return on_chip(
        functools.partial(sum_kernel, n, shifts),
        pltpu.VMEM((8, 144, VS), jnp.int16),
        pieces + extra,
        [pltpu.VMEM((256, VS), jnp.float32)],
        12 * 2 * 256**3,
        {} if base is None else {len(pieces): 0},
    )


def last_kernel(parts, out):
    exps = [
        parts[z, 128:144, :].astype(jnp.int32).astype(jnp.float32)[:1] for z in range(8)
    ]
    for r in range(2):
        for b in range(2):
            part = pl.ds((r * 2 + b) * 32, 32)
            total = decoded(parts[0, part, :], exps[0])
            for z in range(1, 8):
                total = total + decoded(parts[z, part, :], exps[z])
            total = total / NSAMP
            for a in range(2):
                out[:, a, r, 0, b, :] = total[a * 16 : (a + 1) * 16]


def last(parts):
    return on_chip(
        last_kernel,
        jax.ShapeDtypeStruct((16, 2, 2, 1, 2, VS), jnp.float32),
        [parts],
        [],
        2 * 256**3,
    )


def on_device(blocks, block_ids, block_counts):
    a, b = relaid(blocks)
    tagged_a, tagged_b, tags = tagged(block_ids.reshape(OCC), block_counts.reshape(1), (a, b))
    up = [rotate(a, "vcol", -1), rotate(tagged_b, "vcol", -1)]
    down = [rotate(tagged_a, "vcol", 1), rotate(b, "vcol", 1)]
    sib = [rotate(a, "vrow", 1), rotate(tagged_b, "vrow", 1)]
    far_tags = rotate(tags, "vcol", 2)
    second = [rotate(up[0], "vcol", -1), rotate(down[1], "vcol", 1)]
    col_tags = [tags, sib[1]]

    def exchanged(pieces):
        return [pieces[0]] + [rotate(pieces[k], "x", k) for k in (1, 2, 3)]

    *here, cols = tables(col_tags, [tags], [a, b, *sib], gathers=True)
    near = tables(col_tags, [up[1], down[0]], [cols, *up, *down])
    far = tables(col_tags, [far_tags], [cols, *second])
    here, near, far = (
        exchanged(pieces) for pieces in (here, near, far)
    )
    parts = summed(((0,), (1, 3)), here + near)
    parts = summed(((2,),), far, parts)
    parts = lax.all_to_all(parts, "z", 0, 0, tiled=True)
    return last(parts)


def solution(mesh):
    fine = Mesh(mesh.devices.reshape(-1, NX, 2, 4), ("z", "x", "vrow", "vcol"))
    field = ("z", "x")
    held = (
        P(("vrow", "vcol"), field, None, None),
        P(("vrow", "vcol"), field, None),
        P(("vrow", "vcol"), field),
    )
    return jax.shard_map(
        on_device,
        mesh=fine,
        in_specs=held,
        out_specs=P(("vrow", *field), None, None, "vcol", None, None),
        check_vma=False,
    )
```

profile of v0, /device:TPU:2, one launch (start us, length us, event | category | flops | bytes accessed | tf_op | source)
XLA Modules:
  0.0 71.9 jit_solution(12714087884884992601)
XLA Ops:
  0.0 1.3 %shard_map.37 = (bf16[768,256]{1,0:T(8,128)(2,1)S(1)}, bf16[768,256]{1,0:T(8,128)(2,1)S(1)}) custom-call(bf16[128,6,2,256]{3,2,1,0:T(2,128)(2,1)} %blocks.1), custom_call_target="tpu_custom_call" | custom-call | tf_op jit(solution)/shard_map/pallas_call | solution.py:82
  1.4 0.1 collective-permute-start.2
  1.5 3.1 %collective-permute-start.3 = (bf16[768,256]{1,0:T(8,128)(2,1)S(1)}, bf16[768,256]{1,0:T(8,128)(2,1)S(1)}, u32[]{:S(2)}, u32[]{:S(2)}) collective-permute-start(bf16[768,256]{1,0:T(8,128)(2,1)S(1)} %get-tuple-element.23.a.refs_3_), channel_id=1, source_target_pairs={{0,3},{1,0},{2,1},{3,2},{4,7},{5,4},{6,5},{7,6},{8,11},{9,8},{10,9... | collective-permute-start | bytes 1179656 | tf_op jit(solution)/shard_map/ppermute | solution.py:46
  4.5 0.0 collective-permute-start.5
  5.2 0.0 copy-start
  5.2 0.6 copy-done
  5.9 0.6 shard_map.38
  6.5 0.2 collective-permute-start
  6.7 3.2 %collective-permute-start.13 = (bf16[784,256]{1,0:T(8,128)(2,1)S(1)}, bf16[784,256]{1,0:T(8,128)(2,1)S(1)}, u32[]{:S(2)}, u32[]{:S(2)}) collective-permute-start(bf16[784,256]{1,0:T(8,128)(2,1)S(1)} %get-tuple-element.26), channel_id=1, source_target_pairs={{0,3},{1,0},{2,1},{3,2},{4,7},{5,4},{6,5},{7,6},{8,11},{9,8},{10,9... | collective-permute-start | bytes 1204232 | tf_op jit(solution)/shard_map/ppermute | solution.py:46
  9.9 0.0 collective-permute-done.2.refs_5_
  9.9 0.0 collective-permute-start.14
  9.9 4.2 %collective-permute-done.3.refs_5_ = bf16[768,256]{1,0:T(8,128)(2,1)S(1)} collective-permute-done((bf16[768,256]{1,0:T(8,128)(2,1)S(1)}, bf16[768,256]{1,0:T(8,128)(2,1)S(1)}, u32[]{:S(2)}, u32[]{:S(2)}) %collective-permute-start.3) | collective-permute-done | bytes 393248 | tf_op jit(solution)/shard_map/ppermute | solution.py:46
  14.1 3.7 %collective-permute-start.4 = (bf16[768,256]{1,0:T(8,128)(2,1)S(1)}, bf16[768,256]{1,0:T(8,128)(2,1)S(1)}, u32[]{:S(2)}, u32[]{:S(2)}) collective-permute-start(bf16[768,256]{1,0:T(8,128)(2,1)S(1)} %collective-permute-done.3.refs_5_), channel_id=1, source_target_pairs={{0,3},{1,0},{2,1},{3,2},{4,7},{5,4},{6,5},{7,6},{8,11},{9,8},{10,9... | collective-permute-start | bytes 1179656 | tf_op jit(solution)/shard_map/ppermute | solution.py:46
  17.7 0.0 collective-permute-done.5.refs_8_
  17.7 0.0 collective-permute-start.6
  17.8 0.0 collective-permute-done.refs_1_.refs_6_
  17.8 1.0 %shard_map.39 = (f32[1,256,128]{2,1,0:T(8,128)S(1)}, s16[1,272,128]{2,1,0:T(8,128)(2,1)S(1)}, s16[1,272,128]{2,1,0:T(8,128)(2,1)S(1)}, s16[1,272,128]{2,1,0:T(8,128)(2,1)S(1)}, bf16[2,6,256,256]{3,2,1,0:T(8,128)(2,1)S(1)}) custom-call(bf16[16,256]{1,0:T(8,128)(2,1)S(1)} %get-tuple-element.25.refs_0_.refs_2_, ...), custom_call_target="tpu_custom_call" | custom-call | flops 402653184 | tf_op jit(solution)/shard_map/pallas_call | solution.py:32
  18.8 1.6 %collective-permute-start.10 = (s16[1,272,128]{2,1,0:T(8,128)(2,1)S(1)}, s16[1,272,128]{2,1,0:T(8,128)(2,1)S(1)}, u32[]{:S(2)}, u32[]{:S(2)}) collective-permute-start(s16[1,272,128]{2,1,0:T(8,128)(2,1)S(1)} %get-tuple-element.33), channel_id=1, source_target_pairs={{0,8},{8,16},{16,24},{24,0},{1,9},{9,17},{17,25},{25,1},{2,10},{10... | collective-permute-start | bytes 208904 | tf_op jit(solution)/shard_map/ppermute | solution.py:46
  20.4 2.3 %collective-permute-done.13.refs_2_.refs_6_ = bf16[784,256]{1,0:T(8,128)(2,1)S(1)} collective-permute-done((bf16[784,256]{1,0:T(8,128)(2,1)S(1)}, bf16[784,256]{1,0:T(8,128)(2,1)S(1)}, u32[]{:S(2)}, u32[]{:S(2)}) %collective-permute-start.13) | collective-permute-done | bytes 401440 | tf_op jit(solution)/shard_map/ppermute | solution.py:46
  22.7 3.7 %collective-permute-done.14.refs_3_.refs_7_ = bf16[784,256]{1,0:T(8,128)(2,1)S(1)} collective-permute-done((bf16[784,256]{1,0:T(8,128)(2,1)S(1)}, bf16[784,256]{1,0:T(8,128)(2,1)S(1)}, u32[]{:S(2)}, u32[]{:S(2)}) %collective-permute-start.14) | collective-permute-done | bytes 401440 | tf_op jit(solution)/shard_map/ppermute | solution.py:46
  26.3 1.5 %shard_map.41 = (f32[2,256,128]{2,1,0:T(8,128)S(1)}, s16[2,272,128]{2,1,0:T(8,128)(2,1)S(1)}, s16[2,272,128]{2,1,0:T(8,128)(2,1)S(1)}, s16[2,272,128]{2,1,0:T(8,128)(2,1)S(1)}) custom-call(bf16[16,256]{1,0:T(8,128)(2,1)S(1)} %get-tuple-element.25.refs_0_.refs_2_, bf16[784,256]{1,0:T(8,128)(2,1)S(1)} %collective-permute-done.refs_1_.refs_6_, ...), custom_call_target="tpu_custom_call" | custom-call | flops 805306368 | tf_op jit(solution)/shard_map/pallas_call | solution.py:32
  27.9 1.6 %collective-permute-start.15 = (s16[2,272,128]{2,1,0:T(8,128)(2,1)S(1)}, s16[2,272,128]{2,1,0:T(8,128)(2,1)S(1)}, u32[]{:S(2)}, u32[]{:S(2)}) collective-permute-start(s16[2,272,128]{2,1,0:T(8,128)(2,1)S(1)} %get-tuple-element.38), channel_id=1, source_target_pairs={{0,8},{8,16},{16,24},{24,0},{1,9},{9,17},{17,25},{25,1},{2,10},{10... | collective-permute-start | bytes 417800 | tf_op jit(solution)/shard_map/ppermute | solution.py:46
  29.4 0.0 collective-permute-start.1
  29.4 5.2 %collective-permute-done.1.refs_2_ = bf16[16,256]{1,0:T(8,128)(2,1)S(1)} collective-permute-done((bf16[16,256]{1,0:T(8,128)(2,1)S(1)}, bf16[16,256]{1,0:T(8,128)(2,1)S(1)}, u32[]{:S(2)}, u32[]{:S(2)}) %collective-permute-start.1) | collective-permute-done | bytes 8224 | tf_op jit(solution)/shard_map/ppermute | solution.py:46
  34.6 1.2 %collective-permute-start.16 = (s16[2,272,128]{2,1,0:T(8,128)(2,1)S(1)}, s16[2,272,128]{2,1,0:T(8,128)(2,1)S(1)}, u32[]{:S(2)}, u32[]{:S(2)}) collective-permute-start(s16[2,272,128]{2,1,0:T(8,128)(2,1)S(1)} %get-tuple-element.39), channel_id=1, source_target_pairs={{0,16},{8,24},{16,0},{24,8},{1,17},{9,25},{17,1},{25,9},{2,18},{10... | collective-permute-start | bytes 417800 | tf_op jit(solution)/shard_map/ppermute | solution.py:46
  35.8 0.0 collective-permute-done.10.refs_1_
  35.8 2.0 %collective-permute-start.17 = (s16[2,272,128]{2,1,0:T(8,128)(2,1)S(1)}, s16[2,272,128]{2,1,0:T(8,128)(2,1)S(1)}, u32[]{:S(2)}, u32[]{:S(2)}) collective-permute-start(s16[2,272,128]{2,1,0:T(8,128)(2,1)S(1)} %get-tuple-element.40), channel_id=1, source_target_pairs={{0,24},{8,0},{16,8},{24,16},{1,25},{9,1},{17,9},{25,17},{2,26},{10... | collective-permute-start | bytes 417800 | tf_op jit(solution)/shard_map/ppermute | solution.py:46
  37.9 0.0 collective-permute-done.4.refs_4_
  37.9 0.5 collective-permute-start.11
  38.4 0.0 collective-permute-done.6.refs_5_
  38.4 1.5 %collective-permute-start.12 = (s16[1,272,128]{2,1,0:T(8,128)(2,1)S(1)}, s16[1,272,128]{2,1,0:T(8,128)(2,1)S(1)}, u32[]{:S(2)}, u32[]{:S(2)}) collective-permute-start(s16[1,272,128]{2,1,0:T(8,128)(2,1)S(1)} %get-tuple-element.35), channel_id=1, source_target_pairs={{0,24},{8,0},{16,8},{24,16},{1,25},{9,1},{17,9},{25,17},{2,26},{10... | collective-permute-start | bytes 208904 | tf_op jit(solution)/shard_map/ppermute | solution.py:46
  39.9 1.0 %shard_map.40 = (f32[1,256,128]{2,1,0:T(8,128)S(1)}, s16[1,272,128]{2,1,0:T(8,128)(2,1)S(1)}, s16[1,272,128]{2,1,0:T(8,128)(2,1)S(1)}, s16[1,272,128]{2,1,0:T(8,128)(2,1)S(1)}) custom-call(bf16[16,256]{1,0:T(8,128)(2,1)S(1)} %get-tuple-element.25.refs_0_.refs_2_, bf16[784,256]{1,0:T(8,128)(2,1)S(1)} %collective-permute-done.refs_1_.refs_6_, ...), custom_call_target="tpu_custom_call" | custom-call | flops 402653184 | tf_op jit(solution)/shard_map/pallas_call | solution.py:32
  41.0 3.6 %collective-permute-done.11.refs_2_ = s16[1,272,128]{2,1,0:T(8,128)(2,1)S(1)} collective-permute-done((s16[1,272,128]{2,1,0:T(8,128)(2,1)S(1)}, s16[1,272,128]{2,1,0:T(8,128)(2,1)S(1)}, u32[]{:S(2)}, u32[]{:S(2)}) %collective-permute-start.11) | collective-permute-done | bytes 69664 | tf_op jit(solution)/shard_map/ppermute | solution.py:46
  44.6 0.0 collective-permute-start.7
  44.6 0.6 collective-permute-done.12.refs_3_
  45.1 2.1 %collective-permute-start.8 = (s16[1,272,128]{2,1,0:T(8,128)(2,1)S(1)}, s16[1,272,128]{2,1,0:T(8,128)(2,1)S(1)}, u32[]{:S(2)}, u32[]{:S(2)}) collective-permute-start(s16[1,272,128]{2,1,0:T(8,128)(2,1)S(1)} %get-tuple-element.30), channel_id=1, source_target_pairs={{0,16},{8,24},{16,0},{24,8},{1,17},{9,25},{17,1},{25,9},{2,18},{10... | collective-permute-start | bytes 208904 | tf_op jit(solution)/shard_map/ppermute | solution.py:46
  47.3 0.0 collective-permute-done.15.refs_5_
  47.3 1.9 %collective-permute-start.9 = (s16[1,272,128]{2,1,0:T(8,128)(2,1)S(1)}, s16[1,272,128]{2,1,0:T(8,128)(2,1)S(1)}, u32[]{:S(2)}, u32[]{:S(2)}) collective-permute-start(s16[1,272,128]{2,1,0:T(8,128)(2,1)S(1)} %get-tuple-element.31), channel_id=1, source_target_pairs={{0,24},{8,0},{16,8},{24,16},{1,25},{9,1},{17,9},{25,17},{2,26},{10... | collective-permute-start | bytes 208904 | tf_op jit(solution)/shard_map/ppermute | solution.py:46
  49.2 0.0 collective-permute-done.16.refs_6_
  49.2 0.0 collective-permute-done.17.refs_7_
  49.2 0.5 shard_map.42.refs_4_
  49.7 0.0 collective-permute-done.7.refs_1_
  49.7 1.2 %collective-permute-done.8.refs_2_ = s16[1,272,128]{2,1,0:T(8,128)(2,1)S(1)} collective-permute-done((s16[1,272,128]{2,1,0:T(8,128)(2,1)S(1)}, s16[1,272,128]{2,1,0:T(8,128)(2,1)S(1)}, u32[]{:S(2)}, u32[]{:S(2)}) %collective-permute-start.8) | collective-permute-done | bytes 69664 | tf_op jit(solution)/shard_map/ppermute | solution.py:46
  51.0 0.7 %collective-permute-done.9.refs_3_ = s16[1,272,128]{2,1,0:T(8,128)(2,1)S(1)} collective-permute-done((s16[1,272,128]{2,1,0:T(8,128)(2,1)S(1)}, s16[1,272,128]{2,1,0:T(8,128)(2,1)S(1)}, u32[]{:S(2)}, u32[]{:S(2)}) %collective-permute-start.9) | collective-permute-done | bytes 69664 | tf_op jit(solution)/shard_map/ppermute | solution.py:46
  51.7 0.3 shard_map.43
  52.0 19.1 %all_to_all.5.parts = s16[8,144,128]{2,1,0:T(8,128)(2,1)S(1)} all-to-all(s16[8,144,128]{2,1,0:T(8,128)(2,1)S(1)} %shard_map.43), channel_id=1, replica_groups=mesh['z'=8,'x'=4,'vrow'=2,'vcol'=4] {'z'}, dimensions={0} | all-to-all | bytes 589824 | tf_op jit(solution)/shard_map/all_to_all | solution.py:290
  71.1 0.8 %shard_map.44 = f32[16,2,2,1,2,128]{5,4,3,2,1,0:T(2,128)} custom-call(s16[8,144,128]{2,1,0:T(8,128)(2,1)S(1)} %all_to_all.5.parts), custom_call_target="tpu_custom_call" | custom-call | flops 33554432 | tf_op jit(solution)/shard_map/pallas_call | solution.py:32
Async XLA Ops:
  1.4 8.5 %collective-permute-start.2 = (bf16[768,256]{1,0:T(8,128)(2,1)S(1)}, bf16[768,256]{1,0:T(8,128)(2,1)S(1)}, u32[]{:S(2)}, u32[]{:S(2)}) collective-permute-start(bf16[768,256]{1,0:T(8,128)(2,1)S(1)} %get-tuple-element.23.a.refs_3_), channel_id=1, source_target_pairs={{0,4},{4,0},{1,5},{5,1},{2,6},{6,2},{3,7},{7,3},{8,12},{12,8},{9,1... | collective-permute-start | bytes 1179656 | tf_op jit(solution)/shard_map/ppermute | solution.py:46
  1.5 12.6 %collective-permute-start.3 = (bf16[768,256]{1,0:T(8,128)(2,1)S(1)}, bf16[768,256]{1,0:T(8,128)(2,1)S(1)}, u32[]{:S(2)}, u32[]{:S(2)}) collective-permute-start(bf16[768,256]{1,0:T(8,128)(2,1)S(1)} %get-tuple-element.23.a.refs_3_), channel_id=1, source_target_pairs={{0,3},{1,0},{2,1},{3,2},{4,7},{5,4},{6,5},{7,6},{8,11},{9,8},{10,9... | collective-permute-start | bytes 1179656 | tf_op jit(solution)/shard_map/ppermute | solution.py:46
  4.5 13.2 %collective-permute-start.5 = (bf16[768,256]{1,0:T(8,128)(2,1)S(1)}, bf16[768,256]{1,0:T(8,128)(2,1)S(1)}, u32[]{:S(2)}, u32[]{:S(2)}) collective-permute-start(bf16[768,256]{1,0:T(8,128)(2,1)S(1)} %get-tuple-element.24.b.refs_4_), channel_id=1, source_target_pairs={{0,1},{1,2},{2,3},{3,0},{4,5},{5,6},{6,7},{7,4},{8,9},{9,10},{10,1... | collective-permute-start | bytes 1179656 | tf_op jit(solution)/shard_map/ppermute | solution.py:46
  5.2 0.7 copy-start
  6.5 11.3 %collective-permute-start = (bf16[784,256]{1,0:T(8,128)(2,1)S(1)}, bf16[784,256]{1,0:T(8,128)(2,1)S(1)}, u32[]{:S(2)}, u32[]{:S(2)}) collective-permute-start(bf16[784,256]{1,0:T(8,128)(2,1)S(1)} %get-tuple-element.26), channel_id=1, source_target_pairs={{0,4},{4,0},{1,5},{5,1},{2,6},{6,2},{3,7},{7,3},{8,12},{12,8},{9,1... | collective-permute-start | bytes 1204232 | tf_op jit(solution)/shard_map/ppermute | solution.py:46
  6.7 16.0 %collective-permute-start.13 = (bf16[784,256]{1,0:T(8,128)(2,1)S(1)}, bf16[784,256]{1,0:T(8,128)(2,1)S(1)}, u32[]{:S(2)}, u32[]{:S(2)}) collective-permute-start(bf16[784,256]{1,0:T(8,128)(2,1)S(1)} %get-tuple-element.26), channel_id=1, source_target_pairs={{0,3},{1,0},{2,1},{3,2},{4,7},{5,4},{6,5},{7,6},{8,11},{9,8},{10,9... | collective-permute-start | bytes 1204232 | tf_op jit(solution)/shard_map/ppermute | solution.py:46
  9.9 16.5 %collective-permute-start.14 = (bf16[784,256]{1,0:T(8,128)(2,1)S(1)}, bf16[784,256]{1,0:T(8,128)(2,1)S(1)}, u32[]{:S(2)}, u32[]{:S(2)}) collective-permute-start(bf16[784,256]{1,0:T(8,128)(2,1)S(1)} %get-tuple-element.36), channel_id=1, source_target_pairs={{0,1},{1,2},{2,3},{3,0},{4,5},{5,6},{6,7},{7,4},{8,9},{9,10},{10,1... | collective-permute-start | bytes 1204232 | tf_op jit(solution)/shard_map/ppermute | solution.py:46
  14.1 23.8 %collective-permute-start.4 = (bf16[768,256]{1,0:T(8,128)(2,1)S(1)}, bf16[768,256]{1,0:T(8,128)(2,1)S(1)}, u32[]{:S(2)}, u32[]{:S(2)}) collective-permute-start(bf16[768,256]{1,0:T(8,128)(2,1)S(1)} %collective-permute-done.3.refs_5_), channel_id=1, source_target_pairs={{0,3},{1,0},{2,1},{3,2},{4,7},{5,4},{6,5},{7,6},{8,11},{9,8},{10,9... | collective-permute-start | bytes 1179656 | tf_op jit(solution)/shard_map/ppermute | solution.py:46
  17.7 20.7 %collective-permute-start.6 = (bf16[768,256]{1,0:T(8,128)(2,1)S(1)}, bf16[768,256]{1,0:T(8,128)(2,1)S(1)}, u32[]{:S(2)}, u32[]{:S(2)}) collective-permute-start(bf16[768,256]{1,0:T(8,128)(2,1)S(1)} %collective-permute-done.5.refs_8_), channel_id=1, source_target_pairs={{0,1},{1,2},{2,3},{3,0},{4,5},{5,6},{6,7},{7,4},{8,9},{9,10},{10,1... | collective-permute-start | bytes 1179656 | tf_op jit(solution)/shard_map/ppermute | solution.py:46
  18.8 17.0 %collective-permute-start.10 = (s16[1,272,128]{2,1,0:T(8,128)(2,1)S(1)}, s16[1,272,128]{2,1,0:T(8,128)(2,1)S(1)}, u32[]{:S(2)}, u32[]{:S(2)}) collective-permute-start(s16[1,272,128]{2,1,0:T(8,128)(2,1)S(1)} %get-tuple-element.33), channel_id=1, source_target_pairs={{0,8},{8,16},{16,24},{24,0},{1,9},{9,17},{17,25},{25,1},{2,10},{10... | collective-permute-start | bytes 208904 | tf_op jit(solution)/shard_map/ppermute | solution.py:46
  27.9 19.4 %collective-permute-start.15 = (s16[2,272,128]{2,1,0:T(8,128)(2,1)S(1)}, s16[2,272,128]{2,1,0:T(8,128)(2,1)S(1)}, u32[]{:S(2)}, u32[]{:S(2)}) collective-permute-start(s16[2,272,128]{2,1,0:T(8,128)(2,1)S(1)} %get-tuple-element.38), channel_id=1, source_target_pairs={{0,8},{8,16},{16,24},{24,0},{1,9},{9,17},{17,25},{25,1},{2,10},{10... | collective-permute-start | bytes 417800 | tf_op jit(solution)/shard_map/ppermute | solution.py:46
  29.4 5.2 %collective-permute-start.1 = (bf16[16,256]{1,0:T(8,128)(2,1)S(1)}, bf16[16,256]{1,0:T(8,128)(2,1)S(1)}, u32[]{:S(2)}, u32[]{:S(2)}) collective-permute-start(bf16[16,256]{1,0:T(8,128)(2,1)S(1)} %get-tuple-element.25.refs_0_.refs_2_), channel_id=1, source_target_pairs={{0,2},{1,3},{2,0},{3,1},{4,6},{5,7},{6,4},{7,5},{8,10},{9,11},{10,... | collective-permute-start | bytes 24584 | tf_op jit(solution)/shard_map/ppermute | solution.py:46
  34.6 14.6 %collective-permute-start.16 = (s16[2,272,128]{2,1,0:T(8,128)(2,1)S(1)}, s16[2,272,128]{2,1,0:T(8,128)(2,1)S(1)}, u32[]{:S(2)}, u32[]{:S(2)}) collective-permute-start(s16[2,272,128]{2,1,0:T(8,128)(2,1)S(1)} %get-tuple-element.39), channel_id=1, source_target_pairs={{0,16},{8,24},{16,0},{24,8},{1,17},{9,25},{17,1},{25,9},{2,18},{10... | collective-permute-start | bytes 417800 | tf_op jit(solution)/shard_map/ppermute | solution.py:46
  35.8 13.4 %collective-permute-start.17 = (s16[2,272,128]{2,1,0:T(8,128)(2,1)S(1)}, s16[2,272,128]{2,1,0:T(8,128)(2,1)S(1)}, u32[]{:S(2)}, u32[]{:S(2)}) collective-permute-start(s16[2,272,128]{2,1,0:T(8,128)(2,1)S(1)} %get-tuple-element.40), channel_id=1, source_target_pairs={{0,24},{8,0},{16,8},{24,16},{1,25},{9,1},{17,9},{25,17},{2,26},{10... | collective-permute-start | bytes 417800 | tf_op jit(solution)/shard_map/ppermute | solution.py:46
  37.9 6.7 %collective-permute-start.11 = (s16[1,272,128]{2,1,0:T(8,128)(2,1)S(1)}, s16[1,272,128]{2,1,0:T(8,128)(2,1)S(1)}, u32[]{:S(2)}, u32[]{:S(2)}) collective-permute-start(s16[1,272,128]{2,1,0:T(8,128)(2,1)S(1)} %get-tuple-element.34), channel_id=1, source_target_pairs={{0,16},{8,24},{16,0},{24,8},{1,17},{9,25},{17,1},{25,9},{2,18},{10... | collective-permute-start | bytes 208904 | tf_op jit(solution)/shard_map/ppermute | solution.py:46
  38.4 6.7 %collective-permute-start.12 = (s16[1,272,128]{2,1,0:T(8,128)(2,1)S(1)}, s16[1,272,128]{2,1,0:T(8,128)(2,1)S(1)}, u32[]{:S(2)}, u32[]{:S(2)}) collective-permute-start(s16[1,272,128]{2,1,0:T(8,128)(2,1)S(1)} %get-tuple-element.35), channel_id=1, source_target_pairs={{0,24},{8,0},{16,8},{24,16},{1,25},{9,1},{17,9},{25,17},{2,26},{10... | collective-permute-start | bytes 208904 | tf_op jit(solution)/shard_map/ppermute | solution.py:46
  44.6 5.2 %collective-permute-start.7 = (s16[1,272,128]{2,1,0:T(8,128)(2,1)S(1)}, s16[1,272,128]{2,1,0:T(8,128)(2,1)S(1)}, u32[]{:S(2)}, u32[]{:S(2)}) collective-permute-start(s16[1,272,128]{2,1,0:T(8,128)(2,1)S(1)} %get-tuple-element.29), channel_id=1, source_target_pairs={{0,8},{8,16},{16,24},{24,0},{1,9},{9,17},{17,25},{25,1},{2,10},{10... | collective-permute-start | bytes 208904 | tf_op jit(solution)/shard_map/ppermute | solution.py:46
  45.1 5.8 %collective-permute-start.8 = (s16[1,272,128]{2,1,0:T(8,128)(2,1)S(1)}, s16[1,272,128]{2,1,0:T(8,128)(2,1)S(1)}, u32[]{:S(2)}, u32[]{:S(2)}) collective-permute-start(s16[1,272,128]{2,1,0:T(8,128)(2,1)S(1)} %get-tuple-element.30), channel_id=1, source_target_pairs={{0,16},{8,24},{16,0},{24,8},{1,17},{9,25},{17,1},{25,9},{2,18},{10... | collective-permute-start | bytes 208904 | tf_op jit(solution)/shard_map/ppermute | solution.py:46
  47.3 4.4 %collective-permute-start.9 = (s16[1,272,128]{2,1,0:T(8,128)(2,1)S(1)}, s16[1,272,128]{2,1,0:T(8,128)(2,1)S(1)}, u32[]{:S(2)}, u32[]{:S(2)}) collective-permute-start(s16[1,272,128]{2,1,0:T(8,128)(2,1)S(1)} %get-tuple-element.31), channel_id=1, source_target_pairs={{0,24},{8,0},{16,8},{24,16},{1,25},{9,1},{17,9},{25,17},{2,26},{10... | collective-permute-start | bytes 208904 | tf_op jit(solution)/shard_map/ppermute | solution.py:46
where the time goes:
time: 72.4 us; the launch traced here: 71.9 us
  starting transfers between devices  22.8 us (31%)
  waiting for transfers between devices  21.5 us (30%)
  blocking collectives  19.1 us (26%)
  Pallas kernels  7.14 us (10%)
  between operations  0.75 us (1%)
    ppermute x18, starting transfers between devices, rotate(): return lax.ppermute(array, axis, [(i, (i + shift) % n) for i in range(n)])  22.8 us
    ppermute x18, waiting for transfers between devices, rotate(): return lax.ppermute(array, axis, [(i, (i + shift) % n) for i in range(n)])  21.5 us
    all_to_all x1, blocking collectives, on_device(): parts = lax.all_to_all(parts, 'z', 0, 0, tiled=True)  19.1 us
    pallas_call x6, Pallas kernels, on_chip(): pl.pallas_call(f, out_shape=out_shape, in_specs=[VM] * len(arrays), out_s...  5.2 us
  transfers between devices with their start and end apart: 18, of which 8 were waited for; matrix products, arithmetic and copies ran while one was open for 0% of the time, Pallas kernels for 7%

commit v1 on v0

--- a/solution.py
+++ b/solution.py
@@ -43,7 +43,7 @@
 
 def rotate(array, axis, shift):
     n = lax.axis_size(axis)
-    return lax.ppermute(array, axis, [(i, (i + shift) % n) for i in range(n)])
+    return lax.ppermute(array, axis, [(i, i ^ shift) for i in range(n)])
 
 
 def exponent(largest):
@@ -175,7 +175,7 @@
         for s in range(2):
             r = core if s == 0 else 1 - core
             for k in range(NX):
-                there = lax.rem(x + k, NX) * 16
+                there = lax.bitwise_xor(x, k) * 16
                 for zz in range(2):
                     for a in range(2):
                         at = pl.ds(pl.multiple_of(there + a * VS + zz * 64, 16), 16)
@@ -209,7 +209,7 @@
     for g, group in enumerate(shifts):
         mine = ins[g * NX : g * NX + NX]
         for j, shift in enumerate(group):
-            p = lax.rem(y + shift, 4)
+            p = lax.bitwise_xor(y, shift)
             exps = [mine[k][j, 256:272, :].astype(jnp.int32).astype(jnp.float32)[:1] for k in range(1, NX)]
             largest = None
             for rb in range(4):
@@ -269,11 +269,11 @@
 def on_device(blocks, block_ids, block_counts):
     a, b = relaid(blocks)
     tagged_a, tagged_b, tags = tagged(block_ids.reshape(OCC), block_counts.reshape(1), (a, b))
-    up = [rotate(a, "vcol", -1), rotate(tagged_b, "vcol", -1)]
-    down = [rotate(tagged_a, "vcol", 1), rotate(b, "vcol", 1)]
+    up = [rotate(a, "vcol", 1), rotate(tagged_b, "vcol", 1)]
+    down = [rotate(tagged_a, "vcol", 3), rotate(b, "vcol", 3)]
     sib = [rotate(a, "vrow", 1), rotate(tagged_b, "vrow", 1)]
     far_tags = rotate(tags, "vcol", 2)
-    second = [rotate(up[0], "vcol", -1), rotate(down[1], "vcol", 1)]
+    second = [rotate(up[0], "vcol", 3), rotate(down[1], "vcol", 1)]
     col_tags = [tags, sib[1]]
 
     def exchanged(pieces):

time: 72.4 us -> 73.8 us (1.019)
  blocking collectives: 19.1 us -> 20.7 us
    all_to_all x1, blocking collectives: 19.1 us -> 20.7 us  [on_device(): parts = lax.all_to_all(parts, 'z', 0, 0, tiled=True)]
  transfers between devices with their start and end apart: 18 -> 18, of which waited for: 8 -> 8; matrix products, arithmetic and copies ran while one was open for 0% -> 0% of each run, Pallas kernels for 7% -> 6%
where the time goes in v1:
time: 73.8 us; the launch traced here: 73.7 us
  starting transfers between devices  23.3 us (32%)
  waiting for transfers between devices  21 us (28%)
  blocking collectives  20.7 us (28%)
  Pallas kernels  7.17 us (10%)
  between operations  0.76 us (1%)
    ppermute x18, starting transfers between devices, rotate(): return lax.ppermute(array, axis, [(i, i ^ shift) for i in range(n)])  23.3 us
    ppermute x18, waiting for transfers between devices, rotate(): return lax.ppermute(array, axis, [(i, i ^ shift) for i in range(n)])  21 us
    all_to_all x1, blocking collectives, on_device(): parts = lax.all_to_all(parts, 'z', 0, 0, tiled=True)  20.7 us
    pallas_call x6, Pallas kernels, on_chip(): pl.pallas_call(f, out_shape=out_shape, in_specs=[VM] * len(arrays), out_s...  5.23 us
  transfers between devices with their start and end apart: 18, of which 8 were waited for; matrix products, arithmetic and copies ran while one was open for 0% of the time, Pallas kernels for 6%

profile of v1, /device:TPU:2, one launch (start us, length us, event | category | flops | bytes accessed | tf_op | source)
XLA Modules:
  0.0 73.7 jit_solution(9972079099152816545)
XLA Ops:
  0.0 1.3 %shard_map.37 = (bf16[768,256]{1,0:T(8,128)(2,1)S(1)}, bf16[768,256]{1,0:T(8,128)(2,1)S(1)}) custom-call(bf16[128,6,2,256]{3,2,1,0:T(2,128)(2,1)} %blocks.1), custom_call_target="tpu_custom_call" | custom-call | tf_op jit(solution)/shard_map/pallas_call | solution.py:82
  1.4 0.1 collective-permute-start.2
  1.5 1.7 %collective-permute-start.3 = (bf16[768,256]{1,0:T(8,128)(2,1)S(1)}, bf16[768,256]{1,0:T(8,128)(2,1)S(1)}, u32[]{:S(2)}, u32[]{:S(2)}) collective-permute-start(bf16[768,256]{1,0:T(8,128)(2,1)S(1)} %get-tuple-element.23.a.refs_3_), channel_id=1, source_target_pairs={{0,1},{1,0},{2,3},{3,2},{4,5},{5,4},{6,7},{7,6},{8,9},{9,8},{10,11... | collective-permute-start | bytes 1179656 | tf_op jit(solution)/shard_map/ppermute | solution.py:46
  3.1 2.2 %collective-permute-start.5 = (bf16[768,256]{1,0:T(8,128)(2,1)S(1)}, bf16[768,256]{1,0:T(8,128)(2,1)S(1)}, u32[]{:S(2)}, u32[]{:S(2)}) collective-permute-start(bf16[768,256]{1,0:T(8,128)(2,1)S(1)} %get-tuple-element.24.b.refs_4_), channel_id=1, source_target_pairs={{0,3},{1,2},{2,1},{3,0},{4,7},{5,6},{6,5},{7,4},{8,11},{9,10},{10,... | collective-permute-start | bytes 1179656 | tf_op jit(solution)/shard_map/ppermute | solution.py:46
  6.0 0.0 copy-start
  6.0 0.6 copy-done
  6.6 0.6 shard_map.38
  7.2 0.1 collective-permute-start
  7.3 0.8 %collective-permute-start.13 = (bf16[784,256]{1,0:T(8,128)(2,1)S(1)}, bf16[784,256]{1,0:T(8,128)(2,1)S(1)}, u32[]{:S(2)}, u32[]{:S(2)}) collective-permute-start(bf16[784,256]{1,0:T(8,128)(2,1)S(1)} %get-tuple-element.26), channel_id=1, source_target_pairs={{0,1},{1,0},{2,3},{3,2},{4,5},{5,4},{6,7},{7,6},{8,9},{9,8},{10,11... | collective-permute-start | bytes 1204232 | tf_op jit(solution)/shard_map/ppermute | solution.py:46
  8.1 0.0 collective-permute-done.2.refs_5_
  8.1 0.6 collective-permute-start.14
  8.7 4.8 %collective-permute-done.3.refs_5_ = bf16[768,256]{1,0:T(8,128)(2,1)S(1)} collective-permute-done((bf16[768,256]{1,0:T(8,128)(2,1)S(1)}, bf16[768,256]{1,0:T(8,128)(2,1)S(1)}, u32[]{:S(2)}, u32[]{:S(2)}) %collective-permute-start.3) | collective-permute-done | bytes 393248 | tf_op jit(solution)/shard_map/ppermute | solution.py:46
  13.5 3.0 %collective-permute-start.4 = (bf16[768,256]{1,0:T(8,128)(2,1)S(1)}, bf16[768,256]{1,0:T(8,128)(2,1)S(1)}, u32[]{:S(2)}, u32[]{:S(2)}) collective-permute-start(bf16[768,256]{1,0:T(8,128)(2,1)S(1)} %collective-permute-done.3.refs_5_), channel_id=1, source_target_pairs={{0,3},{1,2},{2,1},{3,0},{4,7},{5,6},{6,5},{7,4},{8,11},{9,10},{10,... | collective-permute-start | bytes 1179656 | tf_op jit(solution)/shard_map/ppermute | solution.py:46
  16.5 0.0 collective-permute-done.5.refs_8_
  16.5 0.1 collective-permute-start.6
  16.7 0.0 collective-permute-done.refs_1_.refs_6_
  16.7 1.0 %shard_map.39 = (f32[1,256,128]{2,1,0:T(8,128)S(1)}, s16[1,272,128]{2,1,0:T(8,128)(2,1)S(1)}, s16[1,272,128]{2,1,0:T(8,128)(2,1)S(1)}, s16[1,272,128]{2,1,0:T(8,128)(2,1)S(1)}, bf16[2,6,256,256]{3,2,1,0:T(8,128)(2,1)S(1)}) custom-call(bf16[16,256]{1,0:T(8,128)(2,1)S(1)} %get-tuple-element.25.refs_0_.refs_2_, ...), custom_call_target="tpu_custom_call" | custom-call | flops 402653184 | tf_op jit(solution)/shard_map/pallas_call | solution.py:32
  17.7 1.2 %collective-permute-start.10 = (s16[1,272,128]{2,1,0:T(8,128)(2,1)S(1)}, s16[1,272,128]{2,1,0:T(8,128)(2,1)S(1)}, u32[]{:S(2)}, u32[]{:S(2)}) collective-permute-start(s16[1,272,128]{2,1,0:T(8,128)(2,1)S(1)} %get-tuple-element.33), channel_id=1, source_target_pairs={{0,8},{8,0},{16,24},{24,16},{1,9},{9,1},{17,25},{25,17},{2,10},{10... | collective-permute-start | bytes 208904 | tf_op jit(solution)/shard_map/ppermute | solution.py:46
  18.9 3.2 %collective-permute-done.13.refs_2_.refs_6_ = bf16[784,256]{1,0:T(8,128)(2,1)S(1)} collective-permute-done((bf16[784,256]{1,0:T(8,128)(2,1)S(1)}, bf16[784,256]{1,0:T(8,128)(2,1)S(1)}, u32[]{:S(2)}, u32[]{:S(2)}) %collective-permute-start.13) | collective-permute-done | bytes 401440 | tf_op jit(solution)/shard_map/ppermute | solution.py:46
  22.1 2.8 %collective-permute-done.14.refs_3_.refs_7_ = bf16[784,256]{1,0:T(8,128)(2,1)S(1)} collective-permute-done((bf16[784,256]{1,0:T(8,128)(2,1)S(1)}, bf16[784,256]{1,0:T(8,128)(2,1)S(1)}, u32[]{:S(2)}, u32[]{:S(2)}) %collective-permute-start.14) | collective-permute-done | bytes 401440 | tf_op jit(solution)/shard_map/ppermute | solution.py:46
  24.9 1.5 %shard_map.41 = (f32[2,256,128]{2,1,0:T(8,128)S(1)}, s16[2,272,128]{2,1,0:T(8,128)(2,1)S(1)}, s16[2,272,128]{2,1,0:T(8,128)(2,1)S(1)}, s16[2,272,128]{2,1,0:T(8,128)(2,1)S(1)}) custom-call(bf16[16,256]{1,0:T(8,128)(2,1)S(1)} %get-tuple-element.25.refs_0_.refs_2_, bf16[784,256]{1,0:T(8,128)(2,1)S(1)} %collective-permute-done.refs_1_.refs_6_, ...), custom_call_target="tpu_custom_call" | custom-call | flops 805306368 | tf_op jit(solution)/shard_map/pallas_call | solution.py:32
  26.5 0.8 %collective-permute-start.15 = (s16[2,272,128]{2,1,0:T(8,128)(2,1)S(1)}, s16[2,272,128]{2,1,0:T(8,128)(2,1)S(1)}, u32[]{:S(2)}, u32[]{:S(2)}) collective-permute-start(s16[2,272,128]{2,1,0:T(8,128)(2,1)S(1)} %get-tuple-element.38), channel_id=1, source_target_pairs={{0,8},{8,0},{16,24},{24,16},{1,9},{9,1},{17,25},{25,17},{2,10},{10... | collective-permute-start | bytes 417800 | tf_op jit(solution)/shard_map/ppermute | solution.py:46
  27.3 1.5 %collective-permute-start.1 = (bf16[16,256]{1,0:T(8,128)(2,1)S(1)}, bf16[16,256]{1,0:T(8,128)(2,1)S(1)}, u32[]{:S(2)}, u32[]{:S(2)}) collective-permute-start(bf16[16,256]{1,0:T(8,128)(2,1)S(1)} %get-tuple-element.25.refs_0_.refs_2_), channel_id=1, source_target_pairs={{0,2},{1,3},{2,0},{3,1},{4,6},{5,7},{6,4},{7,5},{8,10},{9,11},{10,... | collective-permute-start | bytes 24584 | tf_op jit(solution)/shard_map/ppermute | solution.py:46
  28.8 3.9 %collective-permute-done.1.refs_2_ = bf16[16,256]{1,0:T(8,128)(2,1)S(1)} collective-permute-done((bf16[16,256]{1,0:T(8,128)(2,1)S(1)}, bf16[16,256]{1,0:T(8,128)(2,1)S(1)}, u32[]{:S(2)}, u32[]{:S(2)}) %collective-permute-start.1) | collective-permute-done | bytes 8224 | tf_op jit(solution)/shard_map/ppermute | solution.py:46
  32.7 2.1 %collective-permute-start.16 = (s16[2,272,128]{2,1,0:T(8,128)(2,1)S(1)}, s16[2,272,128]{2,1,0:T(8,128)(2,1)S(1)}, u32[]{:S(2)}, u32[]{:S(2)}) collective-permute-start(s16[2,272,128]{2,1,0:T(8,128)(2,1)S(1)} %get-tuple-element.39), channel_id=1, source_target_pairs={{0,16},{8,24},{16,0},{24,8},{1,17},{9,25},{17,1},{25,9},{2,18},{10... | collective-permute-start | bytes 417800 | tf_op jit(solution)/shard_map/ppermute | solution.py:46
  34.8 0.0 collective-permute-done.10.refs_1_
  34.8 0.4 collective-permute-start.17
  35.2 0.0 collective-permute-done.4.refs_4_
  35.2 3.3 %collective-permute-start.11 = (s16[1,272,128]{2,1,0:T(8,128)(2,1)S(1)}, s16[1,272,128]{2,1,0:T(8,128)(2,1)S(1)}, u32[]{:S(2)}, u32[]{:S(2)}) collective-permute-start(s16[1,272,128]{2,1,0:T(8,128)(2,1)S(1)} %get-tuple-element.34), channel_id=1, source_target_pairs={{0,16},{8,24},{16,0},{24,8},{1,17},{9,25},{17,1},{25,9},{2,18},{10... | collective-permute-start | bytes 208904 | tf_op jit(solution)/shard_map/ppermute | solution.py:46
  38.6 0.0 collective-permute-done.6.refs_5_
  38.6 0.3 collective-permute-start.12
  38.9 1.0 %shard_map.40 = (f32[1,256,128]{2,1,0:T(8,128)S(1)}, s16[1,272,128]{2,1,0:T(8,128)(2,1)S(1)}, s16[1,272,128]{2,1,0:T(8,128)(2,1)S(1)}, s16[1,272,128]{2,1,0:T(8,128)(2,1)S(1)}) custom-call(bf16[16,256]{1,0:T(8,128)(2,1)S(1)} %get-tuple-element.25.refs_0_.refs_2_, bf16[784,256]{1,0:T(8,128)(2,1)S(1)} %collective-permute-done.refs_1_.refs_6_, ...), custom_call_target="tpu_custom_call" | custom-call | flops 402653184 | tf_op jit(solution)/shard_map/pallas_call | solution.py:32
  39.9 1.1 %collective-permute-done.11.refs_2_ = s16[1,272,128]{2,1,0:T(8,128)(2,1)S(1)} collective-permute-done((s16[1,272,128]{2,1,0:T(8,128)(2,1)S(1)}, s16[1,272,128]{2,1,0:T(8,128)(2,1)S(1)}, u32[]{:S(2)}, u32[]{:S(2)}) %collective-permute-start.11) | collective-permute-done | bytes 69664 | tf_op jit(solution)/shard_map/ppermute | solution.py:46
  41.0 2.3 %collective-permute-start.7 = (s16[1,272,128]{2,1,0:T(8,128)(2,1)S(1)}, s16[1,272,128]{2,1,0:T(8,128)(2,1)S(1)}, u32[]{:S(2)}, u32[]{:S(2)}) collective-permute-start(s16[1,272,128]{2,1,0:T(8,128)(2,1)S(1)} %get-tuple-element.29), channel_id=1, source_target_pairs={{0,8},{8,0},{16,24},{24,16},{1,9},{9,1},{17,25},{25,17},{2,10},{10... | collective-permute-start | bytes 208904 | tf_op jit(solution)/shard_map/ppermute | solution.py:46
  43.3 1.6 %collective-permute-done.12.refs_3_ = s16[1,272,128]{2,1,0:T(8,128)(2,1)S(1)} collective-permute-done((s16[1,272,128]{2,1,0:T(8,128)(2,1)S(1)}, s16[1,272,128]{2,1,0:T(8,128)(2,1)S(1)}, u32[]{:S(2)}, u32[]{:S(2)}) %collective-permute-start.12) | collective-permute-done | bytes 69664 | tf_op jit(solution)/shard_map/ppermute | solution.py:46
  44.9 2.1 %collective-permute-start.8 = (s16[1,272,128]{2,1,0:T(8,128)(2,1)S(1)}, s16[1,272,128]{2,1,0:T(8,128)(2,1)S(1)}, u32[]{:S(2)}, u32[]{:S(2)}) collective-permute-start(s16[1,272,128]{2,1,0:T(8,128)(2,1)S(1)} %get-tuple-element.30), channel_id=1, source_target_pairs={{0,16},{8,24},{16,0},{24,8},{1,17},{9,25},{17,1},{25,9},{2,18},{10... | collective-permute-start | bytes 208904 | tf_op jit(solution)/shard_map/ppermute | solution.py:46
  47.1 0.0 collective-permute-done.15.refs_5_
  47.1 0.7 collective-permute-start.9
  47.7 0.0 collective-permute-done.16.refs_6_
  47.7 0.0 collective-permute-done.17.refs_7_
  47.7 0.5 shard_map.42.refs_4_
  48.3 0.0 collective-permute-done.7.refs_1_
  48.3 2.4 %collective-permute-done.8.refs_2_ = s16[1,272,128]{2,1,0:T(8,128)(2,1)S(1)} collective-permute-done((s16[1,272,128]{2,1,0:T(8,128)(2,1)S(1)}, s16[1,272,128]{2,1,0:T(8,128)(2,1)S(1)}, u32[]{:S(2)}, u32[]{:S(2)}) %collective-permute-start.8) | collective-permute-done | bytes 69664 | tf_op jit(solution)/shard_map/ppermute | solution.py:46
  50.8 1.1 %collective-permute-done.9.refs_3_ = s16[1,272,128]{2,1,0:T(8,128)(2,1)S(1)} collective-permute-done((s16[1,272,128]{2,1,0:T(8,128)(2,1)S(1)}, s16[1,272,128]{2,1,0:T(8,128)(2,1)S(1)}, u32[]{:S(2)}, u32[]{:S(2)}) %collective-permute-start.9) | collective-permute-done | bytes 69664 | tf_op jit(solution)/shard_map/ppermute | solution.py:46
  51.9 0.3 shard_map.43
  52.1 20.7 %all_to_all.5.parts = s16[8,144,128]{2,1,0:T(8,128)(2,1)S(1)} all-to-all(s16[8,144,128]{2,1,0:T(8,128)(2,1)S(1)} %shard_map.43), channel_id=1, replica_groups=mesh['z'=8,'x'=4,'vrow'=2,'vcol'=4] {'z'}, dimensions={0} | all-to-all | bytes 589824 | tf_op jit(solution)/shard_map/all_to_all | solution.py:290
  72.9 0.8 %shard_map.44 = f32[16,2,2,1,2,128]{5,4,3,2,1,0:T(2,128)} custom-call(s16[8,144,128]{2,1,0:T(8,128)(2,1)S(1)} %all_to_all.5.parts), custom_call_target="tpu_custom_call" | custom-call | flops 33554432 | tf_op jit(solution)/shard_map/pallas_call | solution.py:32
Async XLA Ops:
  1.4 6.7 %collective-permute-start.2 = (bf16[768,256]{1,0:T(8,128)(2,1)S(1)}, bf16[768,256]{1,0:T(8,128)(2,1)S(1)}, u32[]{:S(2)}, u32[]{:S(2)}) collective-permute-start(bf16[768,256]{1,0:T(8,128)(2,1)S(1)} %get-tuple-element.23.a.refs_3_), channel_id=1, source_target_pairs={{0,4},{4,0},{1,5},{5,1},{2,6},{6,2},{3,7},{7,3},{8,12},{12,8},{9,1... | collective-permute-start | bytes 1179656 | tf_op jit(solution)/shard_map/ppermute | solution.py:46
  1.5 12.1 %collective-permute-start.3 = (bf16[768,256]{1,0:T(8,128)(2,1)S(1)}, bf16[768,256]{1,0:T(8,128)(2,1)S(1)}, u32[]{:S(2)}, u32[]{:S(2)}) collective-permute-start(bf16[768,256]{1,0:T(8,128)(2,1)S(1)} %get-tuple-element.23.a.refs_3_), channel_id=1, source_target_pairs={{0,1},{1,0},{2,3},{3,2},{4,5},{5,4},{6,7},{7,6},{8,9},{9,8},{10,11... | collective-permute-start | bytes 1179656 | tf_op jit(solution)/shard_map/ppermute | solution.py:46
  3.1 13.4 %collective-permute-start.5 = (bf16[768,256]{1,0:T(8,128)(2,1)S(1)}, bf16[768,256]{1,0:T(8,128)(2,1)S(1)}, u32[]{:S(2)}, u32[]{:S(2)}) collective-permute-start(bf16[768,256]{1,0:T(8,128)(2,1)S(1)} %get-tuple-element.24.b.refs_4_), channel_id=1, source_target_pairs={{0,3},{1,2},{2,1},{3,0},{4,7},{5,6},{6,5},{7,4},{8,11},{9,10},{10,... | collective-permute-start | bytes 1179656 | tf_op jit(solution)/shard_map/ppermute | solution.py:46
  6.0 0.7 copy-start
  7.2 9.5 %collective-permute-start = (bf16[784,256]{1,0:T(8,128)(2,1)S(1)}, bf16[784,256]{1,0:T(8,128)(2,1)S(1)}, u32[]{:S(2)}, u32[]{:S(2)}) collective-permute-start(bf16[784,256]{1,0:T(8,128)(2,1)S(1)} %get-tuple-element.26), channel_id=1, source_target_pairs={{0,4},{4,0},{1,5},{5,1},{2,6},{6,2},{3,7},{7,3},{8,12},{12,8},{9,1... | collective-permute-start | bytes 1204232 | tf_op jit(solution)/shard_map/ppermute | solution.py:46
  7.3 14.8 %collective-permute-start.13 = (bf16[784,256]{1,0:T(8,128)(2,1)S(1)}, bf16[784,256]{1,0:T(8,128)(2,1)S(1)}, u32[]{:S(2)}, u32[]{:S(2)}) collective-permute-start(bf16[784,256]{1,0:T(8,128)(2,1)S(1)} %get-tuple-element.26), channel_id=1, source_target_pairs={{0,1},{1,0},{2,3},{3,2},{4,5},{5,4},{6,7},{7,6},{8,9},{9,8},{10,11... | collective-permute-start | bytes 1204232 | tf_op jit(solution)/shard_map/ppermute | solution.py:46
  8.1 16.8 %collective-permute-start.14 = (bf16[784,256]{1,0:T(8,128)(2,1)S(1)}, bf16[784,256]{1,0:T(8,128)(2,1)S(1)}, u32[]{:S(2)}, u32[]{:S(2)}) collective-permute-start(bf16[784,256]{1,0:T(8,128)(2,1)S(1)} %get-tuple-element.36), channel_id=1, source_target_pairs={{0,3},{1,2},{2,1},{3,0},{4,7},{5,6},{6,5},{7,4},{8,11},{9,10},{10,... | collective-permute-start | bytes 1204232 | tf_op jit(solution)/shard_map/ppermute | solution.py:46
  13.5 21.7 %collective-permute-start.4 = (bf16[768,256]{1,0:T(8,128)(2,1)S(1)}, bf16[768,256]{1,0:T(8,128)(2,1)S(1)}, u32[]{:S(2)}, u32[]{:S(2)}) collective-permute-start(bf16[768,256]{1,0:T(8,128)(2,1)S(1)} %collective-permute-done.3.refs_5_), channel_id=1, source_target_pairs={{0,3},{1,2},{2,1},{3,0},{4,7},{5,6},{6,5},{7,4},{8,11},{9,10},{10,... | collective-permute-start | bytes 1179656 | tf_op jit(solution)/shard_map/ppermute | solution.py:46
  16.5 22.0 %collective-permute-start.6 = (bf16[768,256]{1,0:T(8,128)(2,1)S(1)}, bf16[768,256]{1,0:T(8,128)(2,1)S(1)}, u32[]{:S(2)}, u32[]{:S(2)}) collective-permute-start(bf16[768,256]{1,0:T(8,128)(2,1)S(1)} %collective-permute-done.5.refs_8_), channel_id=1, source_target_pairs={{0,1},{1,0},{2,3},{3,2},{4,5},{5,4},{6,7},{7,6},{8,9},{9,8},{10,11... | collective-permute-start | bytes 1179656 | tf_op jit(solution)/shard_map/ppermute | solution.py:46
  17.7 17.1 %collective-permute-start.10 = (s16[1,272,128]{2,1,0:T(8,128)(2,1)S(1)}, s16[1,272,128]{2,1,0:T(8,128)(2,1)S(1)}, u32[]{:S(2)}, u32[]{:S(2)}) collective-permute-start(s16[1,272,128]{2,1,0:T(8,128)(2,1)S(1)} %get-tuple-element.33), channel_id=1, source_target_pairs={{0,8},{8,0},{16,24},{24,16},{1,9},{9,1},{17,25},{25,17},{2,10},{10... | collective-permute-start | bytes 208904 | tf_op jit(solution)/shard_map/ppermute | solution.py:46
  26.5 20.6 %collective-permute-start.15 = (s16[2,272,128]{2,1,0:T(8,128)(2,1)S(1)}, s16[2,272,128]{2,1,0:T(8,128)(2,1)S(1)}, u32[]{:S(2)}, u32[]{:S(2)}) collective-permute-start(s16[2,272,128]{2,1,0:T(8,128)(2,1)S(1)} %get-tuple-element.38), channel_id=1, source_target_pairs={{0,8},{8,0},{16,24},{24,16},{1,9},{9,1},{17,25},{25,17},{2,10},{10... | collective-permute-start | bytes 417800 | tf_op jit(solution)/shard_map/ppermute | solution.py:46
  27.3 5.4 %collective-permute-start.1 = (bf16[16,256]{1,0:T(8,128)(2,1)S(1)}, bf16[16,256]{1,0:T(8,128)(2,1)S(1)}, u32[]{:S(2)}, u32[]{:S(2)}) collective-permute-start(bf16[16,256]{1,0:T(8,128)(2,1)S(1)} %get-tuple-element.25.refs_0_.refs_2_), channel_id=1, source_target_pairs={{0,2},{1,3},{2,0},{3,1},{4,6},{5,7},{6,4},{7,5},{8,10},{9,11},{10,... | collective-permute-start | bytes 24584 | tf_op jit(solution)/shard_map/ppermute | solution.py:46
  32.7 15.1 %collective-permute-start.16 = (s16[2,272,128]{2,1,0:T(8,128)(2,1)S(1)}, s16[2,272,128]{2,1,0:T(8,128)(2,1)S(1)}, u32[]{:S(2)}, u32[]{:S(2)}) collective-permute-start(s16[2,272,128]{2,1,0:T(8,128)(2,1)S(1)} %get-tuple-element.39), channel_id=1, source_target_pairs={{0,16},{8,24},{16,0},{24,8},{1,17},{9,25},{17,1},{25,9},{2,18},{10... | collective-permute-start | bytes 417800 | tf_op jit(solution)/shard_map/ppermute | solution.py:46
  34.8 12.9 %collective-permute-start.17 = (s16[2,272,128]{2,1,0:T(8,128)(2,1)S(1)}, s16[2,272,128]{2,1,0:T(8,128)(2,1)S(1)}, u32[]{:S(2)}, u32[]{:S(2)}) collective-permute-start(s16[2,272,128]{2,1,0:T(8,128)(2,1)S(1)} %get-tuple-element.40), channel_id=1, source_target_pairs={{0,24},{8,16},{16,8},{24,0},{1,25},{9,17},{17,9},{25,1},{2,26},{10... | collective-permute-start | bytes 417800 | tf_op jit(solution)/shard_map/ppermute | solution.py:46
  35.2 5.8 %collective-permute-start.11 = (s16[1,272,128]{2,1,0:T(8,128)(2,1)S(1)}, s16[1,272,128]{2,1,0:T(8,128)(2,1)S(1)}, u32[]{:S(2)}, u32[]{:S(2)}) collective-permute-start(s16[1,272,128]{2,1,0:T(8,128)(2,1)S(1)} %get-tuple-element.34), channel_id=1, source_target_pairs={{0,16},{8,24},{16,0},{24,8},{1,17},{9,25},{17,1},{25,9},{2,18},{10... | collective-permute-start | bytes 208904 | tf_op jit(solution)/shard_map/ppermute | solution.py:46
  38.6 6.4 %collective-permute-start.12 = (s16[1,272,128]{2,1,0:T(8,128)(2,1)S(1)}, s16[1,272,128]{2,1,0:T(8,128)(2,1)S(1)}, u32[]{:S(2)}, u32[]{:S(2)}) collective-permute-start(s16[1,272,128]{2,1,0:T(8,128)(2,1)S(1)} %get-tuple-element.35), channel_id=1, source_target_pairs={{0,24},{8,16},{16,8},{24,0},{1,25},{9,17},{17,9},{25,1},{2,26},{10... | collective-permute-start | bytes 208904 | tf_op jit(solution)/shard_map/ppermute | solution.py:46
  41.0 7.3 %collective-permute-start.7 = (s16[1,272,128]{2,1,0:T(8,128)(2,1)S(1)}, s16[1,272,128]{2,1,0:T(8,128)(2,1)S(1)}, u32[]{:S(2)}, u32[]{:S(2)}) collective-permute-start(s16[1,272,128]{2,1,0:T(8,128)(2,1)S(1)} %get-tuple-element.29), channel_id=1, source_target_pairs={{0,8},{8,0},{16,24},{24,16},{1,9},{9,1},{17,25},{25,17},{2,10},{10... | collective-permute-start | bytes 208904 | tf_op jit(solution)/shard_map/ppermute | solution.py:46
  44.9 5.8 %collective-permute-start.8 = (s16[1,272,128]{2,1,0:T(8,128)(2,1)S(1)}, s16[1,272,128]{2,1,0:T(8,128)(2,1)S(1)}, u32[]{:S(2)}, u32[]{:S(2)}) collective-permute-start(s16[1,272,128]{2,1,0:T(8,128)(2,1)S(1)} %get-tuple-element.30), channel_id=1, source_target_pairs={{0,16},{8,24},{16,0},{24,8},{1,17},{9,25},{17,1},{25,9},{2,18},{10... | collective-permute-start | bytes 208904 | tf_op jit(solution)/shard_map/ppermute | solution.py:46
  47.1 4.8 %collective-permute-start.9 = (s16[1,272,128]{2,1,0:T(8,128)(2,1)S(1)}, s16[1,272,128]{2,1,0:T(8,128)(2,1)S(1)}, u32[]{:S(2)}, u32[]{:S(2)}) collective-permute-start(s16[1,272,128]{2,1,0:T(8,128)(2,1)S(1)} %get-tuple-element.31), channel_id=1, source_target_pairs={{0,24},{8,16},{16,8},{24,0},{1,25},{9,17},{17,9},{25,1},{2,26},{10... | collective-permute-start | bytes 208904 | tf_op jit(solution)/shard_map/ppermute | solution.py:46

commit v2 on v1

--- a/solution.py
+++ b/solution.py
@@ -203,54 +203,72 @@
     )
 
 
-def sum_kernel(n, shifts, *refs):
-    ins, (out, acc) = refs[: n * NX], refs[-2:]
-    y = lax.axis_index("vcol")
-    for g, group in enumerate(shifts):
-        mine = ins[g * NX : g * NX + NX]
-        for j, shift in enumerate(group):
-            p = lax.bitwise_xor(y, shift)
-            exps = [mine[k][j, 256:272, :].astype(jnp.int32).astype(jnp.float32)[:1] for k in range(1, NX)]
-            largest = None
+def sum_kernel(n, *refs):
+    mine, (kept, sent) = refs[:NX], refs[NX:]
+    zz = lax.axis_index("zz")
+    for j in range(n):
+        exps = [
+            mine[k][j, 256:272, :].astype(jnp.int32).astype(jnp.float32)[:1] for k in range(1, NX)
+        ]
+        for half, out in ((zz, kept), (1 - zz, sent)):
             for rb in range(4):
-                part = pl.ds(rb * 64, 64)
+                part = pl.ds(pl.multiple_of(rb * 64 + half * 32, 32), 32)
                 total = mine[0][j, part, :]
                 for k in range(1, NX):
                     total = total + decoded(mine[k][j, part, :], exps[k - 1])
-                acc[part, :] = total
-                largest = total if largest is None else jnp.maximum(largest, total)
-            exp = exponent(jnp.full((16, VS), jnp.max(largest), jnp.float32))
-            for zz in range(2):
-                to = 2 * p + zz
-                out[to, 128:144, :] = exp.astype(jnp.int32).astype(jnp.int16)
-                for rb in range(4):
-                    v = acc[pl.ds(rb * 64 + zz * 32, 32), :]
-                    out[to, rb * 32 : rb * 32 + 32, :] = coded(v, exp[:1])
-
-
-def summed(shifts, pieces, base=None):
-    n = len(shifts)
-    extra = [] if base is None else [base]
+                out[j, rb * 32 : rb * 32 + 32, :] = total
+
+
+def summed(pieces):
+    n = pieces[0].shape[0]
     return on_chip(
-        functools.partial(sum_kernel, n, shifts),
-        pltpu.VMEM((8, 144, VS), jnp.int16),
-        pieces + extra,
-        [pltpu.VMEM((256, VS), jnp.float32)],
-        12 * 2 * 256**3,
-        {} if base is None else {len(pieces): 0},
-    )
-
-
-def last_kernel(parts, out):
-    exps = [
-        parts[z, 128:144, :].astype(jnp.int32).astype(jnp.float32)[:1] for z in range(8)
-    ]
+        functools.partial(sum_kernel, n),
+        (pltpu.VMEM((n, 128, VS), jnp.float32),) * 2,
+        pieces,
+        [],
+        n * 4 * 2 * 256**3,
+    )
+
+
+def pair_kernel(shifts, *refs):
+    g = len(shifts)
+    ins, outs, (acc, exps) = refs[: 2 * g], refs[2 * g : 2 * g + 4], refs[2 * g + 4 :]
+    y, zh = lax.axis_index("vcol"), lax.axis_index("zh")
+    for i, group in enumerate(shifts):
+        for j, shift in enumerate(group):
+            p = lax.bitwise_xor(y, shift)
+            total = ins[2 * i][j] + ins[2 * i + 1][j]
+            acc[p] = total
+            exps[p] = exponent(jnp.full((16, VS), jnp.max(total), jnp.float32))
+    outs[0][...] = acc[zh]
+    for m in range(1, 4):
+        p = lax.bitwise_xor(zh, m)
+        exp = exps[p]
+        outs[m][128:144, :] = exp.astype(jnp.int32).astype(jnp.int16)
+        for part in range(4):
+            rows = pl.ds(part * 32, 32)
+            outs[m][rows, :] = coded(acc[p, rows, :], exp[:1])
+
+
+def paired(shifts, pieces):
+    return on_chip(
+        functools.partial(pair_kernel, shifts),
+        (pltpu.VMEM((128, VS), jnp.float32),) + (pltpu.VMEM((144, VS), jnp.int16),) * 3,
+        pieces,
+        [pltpu.VMEM((4, 128, VS), jnp.float32), pltpu.VMEM((4, 16, VS), jnp.float32)],
+        6 * 2 * 256**3,
+    )
+
+
+def last_kernel(*refs):
+    parts, out = refs[:4], refs[4]
+    exps = [parts[m][128:144, :].astype(jnp.int32).astype(jnp.float32)[:1] for m in range(1, 4)]
     for r in range(2):
         for b in range(2):
-            part = pl.ds((r * 2 + b) * 32, 32)
-            total = decoded(parts[0, part, :], exps[0])
-            for z in range(1, 8):
-                total = total + decoded(parts[z, part, :], exps[z])
+            rows = pl.ds((r * 2 + b) * 32, 32)
+            total = parts[0][rows, :]
+            for m in range(1, 4):
+                total = total + decoded(parts[m][rows, :], exps[m - 1])
             total = total / NSAMP
             for a in range(2):
                 out[:, a, r, 0, b, :] = total[a * 16 : (a + 1) * 16]
@@ -260,7 +278,7 @@
     return on_chip(
         last_kernel,
         jax.ShapeDtypeStruct((16, 2, 2, 1, 2, VS), jnp.float32),
-        [parts],
+        parts,
         [],
         2 * 256**3,
     )
@@ -282,18 +300,20 @@
     *here, cols = tables(col_tags, [tags], [a, b, *sib], gathers=True)
     near = tables(col_tags, [up[1], down[0]], [cols, *up, *down])
     far = tables(col_tags, [far_tags], [cols, *second])
-    here, near, far = (
-        exchanged(pieces) for pieces in (here, near, far)
-    )
-    parts = summed(((0,), (1, 3)), here + near)
-    parts = summed(((2,),), far, parts)
-    parts = lax.all_to_all(parts, "z", 0, 0, tiled=True)
-    return last(parts)
+    parts = []
+    for pieces in (here, near, far):
+        pieces = exchanged(pieces)
+        kept, sent = summed(pieces)
+        parts += [kept, rotate(sent, "zz", 1)]
+    kept, *sent = paired(((0,), (1, 3), (2,)), parts)
+    sent = [rotate(sent[m - 1], "zh", m) for m in (1, 2, 3)]
+    return last([kept] + sent)
 
 
 def solution(mesh):
-    fine = Mesh(mesh.devices.reshape(-1, NX, 2, 4), ("z", "x", "vrow", "vcol"))
-    field = ("z", "x")
+    axes = ("zh", "zz", "x", "vrow", "vcol")
+    fine = Mesh(mesh.devices.reshape(-1, 2, NX, 2, 4), axes)
+    field = ("zh", "zz", "x")
     held = (
         P(("vrow", "vcol"), field, None, None),
         P(("vrow", "vcol"), field, None),

time: 73.8 us -> 70.4 us (0.954); the launches traced: 73.7 us -> 69 us
  blocking collectives: 20.7 us -> 0 us
  starting transfers between devices: 23.3 us -> 38.1 us
  waiting for transfers between devices: 21 us -> 22.6 us
    all_to_all x1 -> x0, blocking collectives: 20.7 us -> none  [on_device(): parts = lax.all_to_all(parts, 'z', 0, 0, tiled=True)]
    ppermute x18 -> x24, starting transfers between devices: 23.3 us -> 38.1 us  [rotate(): return lax.ppermute(array, axis, [(i, i ^ shift) for i in range(n)])]
    ppermute x18 -> x24, waiting for transfers between devices: 21 us -> 22.6 us  [rotate(): return lax.ppermute(array, axis, [(i, i ^ shift) for i in range(n)])]
    pallas_call x6 -> x8, Pallas kernels: 5.23 us -> 5.01 us  [on_chip(): pl.pallas_call(f, out_shape=out_shape, in_specs=[VM] * len(arrays), out_s...]
  transfers between devices with their start and end apart: 18 -> 24, of which waited for: 8 -> 10; matrix products, arithmetic and copies ran while one was open for 0% -> 0% of each run, Pallas kernels for 6% -> 7%
where the time goes in v2:
time: 70.4 us; the launch traced here: 69 us
  starting transfers between devices  38.1 us (54%)
  waiting for transfers between devices  22.6 us (32%)
  Pallas kernels  6.95 us (10%)
  between operations  0.78 us (1%)
    ppermute x24, starting transfers between devices, rotate(): return lax.ppermute(array, axis, [(i, i ^ shift) for i in range(n)])  38.1 us
    ppermute x24, waiting for transfers between devices, rotate(): return lax.ppermute(array, axis, [(i, i ^ shift) for i in range(n)])  22.6 us
    pallas_call x8, Pallas kernels, on_chip(): pl.pallas_call(f, out_shape=out_shape, in_specs=[VM] * len(arrays), out_s...  5.01 us
  transfers between devices with their start and end apart: 24, of which 10 were waited for; matrix products, arithmetic and copies ran while one was open for 0% of the time, Pallas kernels for 7%

profile of v2, /device:TPU:2, one launch (start us, length us, event | category | flops | bytes accessed | tf_op | source)
XLA Modules:
  0.0 69.0 jit_solution(7397230861933781202)
XLA Ops:
  0.0 1.3 %shard_map.37 = (bf16[768,256]{1,0:T(8,128)(2,1)S(1)}, bf16[768,256]{1,0:T(8,128)(2,1)S(1)}) custom-call(bf16[128,6,2,256]{3,2,1,0:T(2,128)(2,1)} %blocks.1), custom_call_target="tpu_custom_call" | custom-call | tf_op jit(solution)/shard_map/pallas_call | solution.py:82
  1.4 0.1 collective-permute-start.1
  1.5 1.7 %collective-permute-start.8 = (bf16[768,256]{1,0:T(8,128)(2,1)S(1)}, bf16[768,256]{1,0:T(8,128)(2,1)S(1)}, u32[]{:S(2)}, u32[]{:S(2)}) collective-permute-start(bf16[768,256]{1,0:T(8,128)(2,1)S(1)} %get-tuple-element.33.a.refs_3_), channel_id=1, source_target_pairs={{0,1},{1,0},{2,3},{3,2},{4,5},{5,4},{6,7},{7,6},{8,9},{9,8},{10,11... | collective-permute-start | bytes 1179656 | tf_op jit(solution)/shard_map/ppermute | solution.py:46
  3.1 2.2 %collective-permute-start.9 = (bf16[768,256]{1,0:T(8,128)(2,1)S(1)}, bf16[768,256]{1,0:T(8,128)(2,1)S(1)}, u32[]{:S(2)}, u32[]{:S(2)}) collective-permute-start(bf16[768,256]{1,0:T(8,128)(2,1)S(1)} %get-tuple-element.34.b.refs_4_), channel_id=1, source_target_pairs={{0,3},{1,2},{2,1},{3,0},{4,7},{5,6},{6,5},{7,4},{8,11},{9,10},{10,... | collective-permute-start | bytes 1179656 | tf_op jit(solution)/shard_map/ppermute | solution.py:46
  6.0 0.0 copy-start
  6.0 0.6 copy-done
  6.6 0.6 shard_map.38
  7.2 0.1 collective-permute-start
  7.3 0.8 %collective-permute-start.6 = (bf16[784,256]{1,0:T(8,128)(2,1)S(1)}, bf16[784,256]{1,0:T(8,128)(2,1)S(1)}, u32[]{:S(2)}, u32[]{:S(2)}) collective-permute-start(bf16[784,256]{1,0:T(8,128)(2,1)S(1)} %get-tuple-element.36), channel_id=1, source_target_pairs={{0,1},{1,0},{2,3},{3,2},{4,5},{5,4},{6,7},{7,6},{8,9},{9,8},{10,11... | collective-permute-start | bytes 1204232 | tf_op jit(solution)/shard_map/ppermute | solution.py:46
  8.1 0.0 collective-permute-done.1.refs_5_
  8.1 0.6 collective-permute-start.7
  8.7 4.8 %collective-permute-done.8.refs_5_ = bf16[768,256]{1,0:T(8,128)(2,1)S(1)} collective-permute-done((bf16[768,256]{1,0:T(8,128)(2,1)S(1)}, bf16[768,256]{1,0:T(8,128)(2,1)S(1)}, u32[]{:S(2)}, u32[]{:S(2)}) %collective-permute-start.8) | collective-permute-done | bytes 393248 | tf_op jit(solution)/shard_map/ppermute | solution.py:46
  13.5 3.0 %collective-permute-start.15 = (bf16[768,256]{1,0:T(8,128)(2,1)S(1)}, bf16[768,256]{1,0:T(8,128)(2,1)S(1)}, u32[]{:S(2)}, u32[]{:S(2)}) collective-permute-start(bf16[768,256]{1,0:T(8,128)(2,1)S(1)} %collective-permute-done.8.refs_5_), channel_id=1, source_target_pairs={{0,3},{1,2},{2,1},{3,0},{4,7},{5,6},{6,5},{7,4},{8,11},{9,10},{10,... | collective-permute-start | bytes 1179656 | tf_op jit(solution)/shard_map/ppermute | solution.py:46
  16.5 0.0 collective-permute-done.9.refs_8_
  16.5 0.1 collective-permute-start.16
  16.7 3.3 %collective-permute-start.14 = (bf16[16,256]{1,0:T(8,128)(2,1)S(1)}, bf16[16,256]{1,0:T(8,128)(2,1)S(1)}, u32[]{:S(2)}, u32[]{:S(2)}) collective-permute-start(bf16[16,256]{1,0:T(8,128)(2,1)S(1)} %get-tuple-element.35.refs_0_.refs_2_), channel_id=1, source_target_pairs={{0,2},{1,3},{2,0},{3,1},{4,6},{5,7},{6,4},{7,5},{8,10},{9,11},{10,... | collective-permute-start | bytes 24584 | tf_op jit(solution)/shard_map/ppermute | solution.py:46
  20.0 1.0 %shard_map.39 = (f32[1,256,128]{2,1,0:T(8,128)S(1)}, s16[1,272,128]{2,1,0:T(8,128)(2,1)S(1)}, s16[1,272,128]{2,1,0:T(8,128)(2,1)S(1)}, s16[1,272,128]{2,1,0:T(8,128)(2,1)S(1)}, bf16[2,6,256,256]{3,2,1,0:T(8,128)(2,1)S(1)}) custom-call(bf16[16,256]{1,0:T(8,128)(2,1)S(1)} %get-tuple-element.35.refs_0_.refs_2_, ...), custom_call_target="tpu_custom_call" | custom-call | flops 402653184 | tf_op jit(solution)/shard_map/pallas_call | solution.py:32
  21.0 1.1 %collective-permute-done.6.refs_2_.refs_6_ = bf16[784,256]{1,0:T(8,128)(2,1)S(1)} collective-permute-done((bf16[784,256]{1,0:T(8,128)(2,1)S(1)}, bf16[784,256]{1,0:T(8,128)(2,1)S(1)}, u32[]{:S(2)}, u32[]{:S(2)}) %collective-permute-start.6) | collective-permute-done | bytes 401440 | tf_op jit(solution)/shard_map/ppermute | solution.py:46
  22.1 2.2 %collective-permute-start.2 = (s16[1,272,128]{2,1,0:T(8,128)(2,1)S(1)}, s16[1,272,128]{2,1,0:T(8,128)(2,1)S(1)}, u32[]{:S(2)}, u32[]{:S(2)}) collective-permute-start(s16[1,272,128]{2,1,0:T(8,128)(2,1)S(1)} %get-tuple-element.38), channel_id=1, source_target_pairs={{0,8},{8,0},{16,24},{24,16},{1,9},{9,1},{17,25},{25,17},{2,10},{10... | collective-permute-start | bytes 208904 | tf_op jit(solution)/shard_map/ppermute | solution.py:46
  24.4 0.5 collective-permute-done.7.refs_3_.refs_7_
  24.9 1.6 %shard_map.41 = (f32[2,256,128]{2,1,0:T(8,128)S(1)}, s16[2,272,128]{2,1,0:T(8,128)(2,1)S(1)}, s16[2,272,128]{2,1,0:T(8,128)(2,1)S(1)}, s16[2,272,128]{2,1,0:T(8,128)(2,1)S(1)}) custom-call(bf16[16,256]{1,0:T(8,128)(2,1)S(1)} %get-tuple-element.35.refs_0_.refs_2_, bf16[784,256]{1,0:T(8,128)(2,1)S(1)} %collective-permute-done.refs_1_.refs_6_, ...), custom_call_target="tpu_custom_call" | custom-call | flops 805306368 | tf_op jit(solution)/shard_map/pallas_call | solution.py:32
  26.5 0.8 %collective-permute-start.10 = (s16[2,272,128]{2,1,0:T(8,128)(2,1)S(1)}, s16[2,272,128]{2,1,0:T(8,128)(2,1)S(1)}, u32[]{:S(2)}, u32[]{:S(2)}) collective-permute-start(s16[2,272,128]{2,1,0:T(8,128)(2,1)S(1)} %get-tuple-element.46), channel_id=1, source_target_pairs={{0,8},{8,0},{16,24},{24,16},{1,9},{9,1},{17,25},{25,17},{2,10},{10... | collective-permute-start | bytes 417800 | tf_op jit(solution)/shard_map/ppermute | solution.py:46
  27.3 5.4 %collective-permute-done.14.refs_2_ = bf16[16,256]{1,0:T(8,128)(2,1)S(1)} collective-permute-done((bf16[16,256]{1,0:T(8,128)(2,1)S(1)}, bf16[16,256]{1,0:T(8,128)(2,1)S(1)}, u32[]{:S(2)}, u32[]{:S(2)}) %collective-permute-start.14) | collective-permute-done | bytes 8224 | tf_op jit(solution)/shard_map/ppermute | solution.py:46
  32.7 2.1 %collective-permute-start.11 = (s16[2,272,128]{2,1,0:T(8,128)(2,1)S(1)}, s16[2,272,128]{2,1,0:T(8,128)(2,1)S(1)}, u32[]{:S(2)}, u32[]{:S(2)}) collective-permute-start(s16[2,272,128]{2,1,0:T(8,128)(2,1)S(1)} %get-tuple-element.47), channel_id=1, source_target_pairs={{0,16},{8,24},{16,0},{24,8},{1,17},{9,25},{17,1},{25,9},{2,18},{10... | collective-permute-start | bytes 417800 | tf_op jit(solution)/shard_map/ppermute | solution.py:46
  34.8 3.5 %collective-permute-start.3 = (s16[1,272,128]{2,1,0:T(8,128)(2,1)S(1)}, s16[1,272,128]{2,1,0:T(8,128)(2,1)S(1)}, u32[]{:S(2)}, u32[]{:S(2)}) collective-permute-start(s16[1,272,128]{2,1,0:T(8,128)(2,1)S(1)} %get-tuple-element.39), channel_id=1, source_target_pairs={{0,16},{8,24},{16,0},{24,8},{1,17},{9,25},{17,1},{25,9},{2,18},{10... | collective-permute-start | bytes 208904 | tf_op jit(solution)/shard_map/ppermute | solution.py:46
  38.3 0.5 collective-permute-start.4
  38.9 1.0 %shard_map.43 = (f32[1,256,128]{2,1,0:T(8,128)S(1)}, s16[1,272,128]{2,1,0:T(8,128)(2,1)S(1)}, s16[1,272,128]{2,1,0:T(8,128)(2,1)S(1)}, s16[1,272,128]{2,1,0:T(8,128)(2,1)S(1)}) custom-call(bf16[16,256]{1,0:T(8,128)(2,1)S(1)} %get-tuple-element.35.refs_0_.refs_2_, bf16[784,256]{1,0:T(8,128)(2,1)S(1)} %collective-permute-done.refs_1_.refs_6_, ...), custom_call_target="tpu_custom_call" | custom-call | flops 402653184 | tf_op jit(solution)/shard_map/pallas_call | solution.py:32
  39.9 1.0 %collective-permute-start.17 = (s16[1,272,128]{2,1,0:T(8,128)(2,1)S(1)}, s16[1,272,128]{2,1,0:T(8,128)(2,1)S(1)}, u32[]{:S(2)}, u32[]{:S(2)}) collective-permute-start(s16[1,272,128]{2,1,0:T(8,128)(2,1)S(1)} %get-tuple-element.52), channel_id=1, source_target_pairs={{0,8},{8,0},{16,24},{24,16},{1,9},{9,1},{17,25},{25,17},{2,10},{10... | collective-permute-start | bytes 208904 | tf_op jit(solution)/shard_map/ppermute | solution.py:46
  40.9 0.0 collective-permute-done.11.refs_2_
  40.9 2.2 %collective-permute-start.18 = (s16[1,272,128]{2,1,0:T(8,128)(2,1)S(1)}, s16[1,272,128]{2,1,0:T(8,128)(2,1)S(1)}, u32[]{:S(2)}, u32[]{:S(2)}) collective-permute-start(s16[1,272,128]{2,1,0:T(8,128)(2,1)S(1)} %get-tuple-element.53), channel_id=1, source_target_pairs={{0,16},{8,24},{16,0},{24,8},{1,17},{9,25},{17,1},{25,9},{2,18},{10... | collective-permute-start | bytes 208904 | tf_op jit(solution)/shard_map/ppermute | solution.py:46
  43.1 1.3 %collective-permute-done.12.refs_3_ = s16[2,272,128]{2,1,0:T(8,128)(2,1)S(1)} collective-permute-done((s16[2,272,128]{2,1,0:T(8,128)(2,1)S(1)}, s16[2,272,128]{2,1,0:T(8,128)(2,1)S(1)}, u32[]{:S(2)}, u32[]{:S(2)}) %collective-permute-start.12) | collective-permute-done | bytes 139296 | tf_op jit(solution)/shard_map/ppermute | solution.py:46
  44.5 0.4 collective-permute-start.19
  44.8 0.2 shard_map.42
  45.1 2.0 %collective-permute-start.13 = (f32[2,128,128]{2,1,0:T(8,128)S(1)}, f32[2,128,128]{2,1,0:T(8,128)S(1)}, u32[]{:S(2)}, u32[]{:S(2)}) collective-permute-start(f32[2,128,128]{2,1,0:T(8,128)S(1)} %get-tuple-element.50), channel_id=1, source_target_pairs={{0,32},{32,0},{1,33},{33,1},{2,34},{34,2},{3,35},{35,3},{4,36},{36... | collective-permute-start | bytes 393224 | tf_op jit(solution)/shard_map/ppermute | solution.py:46
  47.1 0.0 collective-permute-done.4.refs_3_
  47.1 0.1 shard_map.40
  47.2 0.6 collective-permute-start.5
  47.8 1.0 %collective-permute-done.19.refs_3_ = s16[1,272,128]{2,1,0:T(8,128)(2,1)S(1)} collective-permute-done((s16[1,272,128]{2,1,0:T(8,128)(2,1)S(1)}, s16[1,272,128]{2,1,0:T(8,128)(2,1)S(1)}, u32[]{:S(2)}, u32[]{:S(2)}) %collective-permute-start.19) | collective-permute-done | bytes 69664 | tf_op jit(solution)/shard_map/ppermute | solution.py:46
  48.8 0.1 shard_map.44
  48.9 2.0 %collective-permute-start.20 = (f32[1,128,128]{2,1,0:T(8,128)S(1)}, f32[1,128,128]{2,1,0:T(8,128)S(1)}, u32[]{:S(2)}, u32[]{:S(2)}) collective-permute-start(f32[1,128,128]{2,1,0:T(8,128)S(1)} %get-tuple-element.56), channel_id=1, source_target_pairs={{0,32},{32,0},{1,33},{33,1},{2,34},{34,2},{3,35},{35,3},{4,36},{36... | collective-permute-start | bytes 196616 | tf_op jit(solution)/shard_map/ppermute | solution.py:46
  50.9 1.1 %collective-permute-done.5.refs_1_ = f32[1,128,128]{2,1,0:T(8,128)S(1)} collective-permute-done((f32[1,128,128]{2,1,0:T(8,128)S(1)}, f32[1,128,128]{2,1,0:T(8,128)S(1)}, u32[]{:S(2)}, u32[]{:S(2)}) %collective-permute-start.5) | collective-permute-done | bytes 65568 | tf_op jit(solution)/shard_map/ppermute | solution.py:46
  52.0 1.2 %collective-permute-done.20.refs_5_ = f32[1,128,128]{2,1,0:T(8,128)S(1)} collective-permute-done((f32[1,128,128]{2,1,0:T(8,128)S(1)}, f32[1,128,128]{2,1,0:T(8,128)S(1)}, u32[]{:S(2)}, u32[]{:S(2)}) %collective-permute-start.20) | collective-permute-done | bytes 65568 | tf_op jit(solution)/shard_map/ppermute | solution.py:46
  53.2 0.2 shard_map.45
  53.5 3.4 %collective-permute-start.21 = (s16[144,128]{1,0:T(8,128)(2,1)S(1)}, s16[144,128]{1,0:T(8,128)(2,1)S(1)}, u32[]{:S(2)}, u32[]{:S(2)}) collective-permute-start(s16[144,128]{1,0:T(8,128)(2,1)S(1)} %get-tuple-element.58), channel_id=1, source_target_pairs={{0,64},{64,0},{128,192},{192,128},{1,65},{65,1},{129,193},{193,129... | collective-permute-start | bytes 110600 | tf_op jit(solution)/shard_map/ppermute | solution.py:46
  56.8 5.4 %collective-permute-start.22 = (s16[144,128]{1,0:T(8,128)(2,1)S(1)}, s16[144,128]{1,0:T(8,128)(2,1)S(1)}, u32[]{:S(2)}, u32[]{:S(2)}) collective-permute-start(s16[144,128]{1,0:T(8,128)(2,1)S(1)} %get-tuple-element.59), channel_id=1, source_target_pairs={{0,128},{64,192},{128,0},{192,64},{1,129},{65,193},{129,1},{193,65... | collective-permute-start | bytes 110600 | tf_op jit(solution)/shard_map/ppermute | solution.py:46
  62.2 2.6 %collective-permute-done.22.refs_2_ = s16[144,128]{1,0:T(8,128)(2,1)S(1)} collective-permute-done((s16[144,128]{1,0:T(8,128)(2,1)S(1)}, s16[144,128]{1,0:T(8,128)(2,1)S(1)}, u32[]{:S(2)}, u32[]{:S(2)}) %collective-permute-start.22) | collective-permute-done | bytes 36896 | tf_op jit(solution)/shard_map/ppermute | solution.py:46
  64.8 3.5 %collective-permute-done.23.refs_3_ = s16[144,128]{1,0:T(8,128)(2,1)S(1)} collective-permute-done((s16[144,128]{1,0:T(8,128)(2,1)S(1)}, s16[144,128]{1,0:T(8,128)(2,1)S(1)}, u32[]{:S(2)}, u32[]{:S(2)}) %collective-permute-start.23) | collective-permute-done | bytes 36896 | tf_op jit(solution)/shard_map/ppermute | solution.py:46
  68.3 0.7 %shard_map.46 = f32[16,2,2,1,2,128]{5,4,3,2,1,0:T(2,128)} custom-call(f32[128,128]{1,0:T(8,128)S(1)} %get-tuple-element.57.refs_0_, s16[144,128]{1,0:T(8,128)(2,1)S(1)} %collective-permute-done.21.refs_1_, s16[144,128]{1,0:T(8,128)(2,1)S(1)} %collective-permute-done.22.refs_2_, s16[144,128]{1,0:T(8,128)(2,1)S(1)} %collective-permute-done.23.refs_3_), custom_call_target="tpu_custom_call" | custom-call | flops 33554432 | tf_op jit(solution)/shard_map/pallas_call | solution.py:32
  (12 shorter events, 0.0 us)
Async XLA Ops:
  1.4 6.7 %collective-permute-start.1 = (bf16[768,256]{1,0:T(8,128)(2,1)S(1)}, bf16[768,256]{1,0:T(8,128)(2,1)S(1)}, u32[]{:S(2)}, u32[]{:S(2)}) collective-permute-start(bf16[768,256]{1,0:T(8,128)(2,1)S(1)} %get-tuple-element.33.a.refs_3_), channel_id=1, source_target_pairs={{0,4},{4,0},{1,5},{5,1},{2,6},{6,2},{3,7},{7,3},{8,12},{12,8},{9,1... | collective-permute-start | bytes 1179656 | tf_op jit(solution)/shard_map/ppermute | solution.py:46
  1.5 12.1 %collective-permute-start.8 = (bf16[768,256]{1,0:T(8,128)(2,1)S(1)}, bf16[768,256]{1,0:T(8,128)(2,1)S(1)}, u32[]{:S(2)}, u32[]{:S(2)}) collective-permute-start(bf16[768,256]{1,0:T(8,128)(2,1)S(1)} %get-tuple-element.33.a.refs_3_), channel_id=1, source_target_pairs={{0,1},{1,0},{2,3},{3,2},{4,5},{5,4},{6,7},{7,6},{8,9},{9,8},{10,11... | collective-permute-start | bytes 1179656 | tf_op jit(solution)/shard_map/ppermute | solution.py:46
  3.1 13.4 %collective-permute-start.9 = (bf16[768,256]{1,0:T(8,128)(2,1)S(1)}, bf16[768,256]{1,0:T(8,128)(2,1)S(1)}, u32[]{:S(2)}, u32[]{:S(2)}) collective-permute-start(bf16[768,256]{1,0:T(8,128)(2,1)S(1)} %get-tuple-element.34.b.refs_4_), channel_id=1, source_target_pairs={{0,3},{1,2},{2,1},{3,0},{4,7},{5,6},{6,5},{7,4},{8,11},{9,10},{10,... | collective-permute-start | bytes 1179656 | tf_op jit(solution)/shard_map/ppermute | solution.py:46
  6.0 0.7 copy-start
  7.2 9.5 %collective-permute-start = (bf16[784,256]{1,0:T(8,128)(2,1)S(1)}, bf16[784,256]{1,0:T(8,128)(2,1)S(1)}, u32[]{:S(2)}, u32[]{:S(2)}) collective-permute-start(bf16[784,256]{1,0:T(8,128)(2,1)S(1)} %get-tuple-element.36), channel_id=1, source_target_pairs={{0,4},{4,0},{1,5},{5,1},{2,6},{6,2},{3,7},{7,3},{8,12},{12,8},{9,1... | collective-permute-start | bytes 1204232 | tf_op jit(solution)/shard_map/ppermute | solution.py:46
  7.3 14.8 %collective-permute-start.6 = (bf16[784,256]{1,0:T(8,128)(2,1)S(1)}, bf16[784,256]{1,0:T(8,128)(2,1)S(1)}, u32[]{:S(2)}, u32[]{:S(2)}) collective-permute-start(bf16[784,256]{1,0:T(8,128)(2,1)S(1)} %get-tuple-element.36), channel_id=1, source_target_pairs={{0,1},{1,0},{2,3},{3,2},{4,5},{5,4},{6,7},{7,6},{8,9},{9,8},{10,11... | collective-permute-start | bytes 1204232 | tf_op jit(solution)/shard_map/ppermute | solution.py:46
  8.1 16.8 %collective-permute-start.7 = (bf16[784,256]{1,0:T(8,128)(2,1)S(1)}, bf16[784,256]{1,0:T(8,128)(2,1)S(1)}, u32[]{:S(2)}, u32[]{:S(2)}) collective-permute-start(bf16[784,256]{1,0:T(8,128)(2,1)S(1)} %get-tuple-element.43), channel_id=1, source_target_pairs={{0,3},{1,2},{2,1},{3,0},{4,7},{5,6},{6,5},{7,4},{8,11},{9,10},{10,... | collective-permute-start | bytes 1204232 | tf_op jit(solution)/shard_map/ppermute | solution.py:46
  13.5 21.3 %collective-permute-start.15 = (bf16[768,256]{1,0:T(8,128)(2,1)S(1)}, bf16[768,256]{1,0:T(8,128)(2,1)S(1)}, u32[]{:S(2)}, u32[]{:S(2)}) collective-permute-start(bf16[768,256]{1,0:T(8,128)(2,1)S(1)} %collective-permute-done.8.refs_5_), channel_id=1, source_target_pairs={{0,3},{1,2},{2,1},{3,0},{4,7},{5,6},{6,5},{7,4},{8,11},{9,10},{10,... | collective-permute-start | bytes 1179656 | tf_op jit(solution)/shard_map/ppermute | solution.py:46
  16.5 21.8 %collective-permute-start.16 = (bf16[768,256]{1,0:T(8,128)(2,1)S(1)}, bf16[768,256]{1,0:T(8,128)(2,1)S(1)}, u32[]{:S(2)}, u32[]{:S(2)}) collective-permute-start(bf16[768,256]{1,0:T(8,128)(2,1)S(1)} %collective-permute-done.9.refs_8_), channel_id=1, source_target_pairs={{0,1},{1,0},{2,3},{3,2},{4,5},{5,4},{6,7},{7,6},{8,9},{9,8},{10,11... | collective-permute-start | bytes 1179656 | tf_op jit(solution)/shard_map/ppermute | solution.py:46
  16.7 16.0 %collective-permute-start.14 = (bf16[16,256]{1,0:T(8,128)(2,1)S(1)}, bf16[16,256]{1,0:T(8,128)(2,1)S(1)}, u32[]{:S(2)}, u32[]{:S(2)}) collective-permute-start(bf16[16,256]{1,0:T(8,128)(2,1)S(1)} %get-tuple-element.35.refs_0_.refs_2_), channel_id=1, source_target_pairs={{0,2},{1,3},{2,0},{3,1},{4,6},{5,7},{6,4},{7,5},{8,10},{9,11},{10,... | collective-permute-start | bytes 24584 | tf_op jit(solution)/shard_map/ppermute | solution.py:46
  22.1 12.7 %collective-permute-start.2 = (s16[1,272,128]{2,1,0:T(8,128)(2,1)S(1)}, s16[1,272,128]{2,1,0:T(8,128)(2,1)S(1)}, u32[]{:S(2)}, u32[]{:S(2)}) collective-permute-start(s16[1,272,128]{2,1,0:T(8,128)(2,1)S(1)} %get-tuple-element.38), channel_id=1, source_target_pairs={{0,8},{8,0},{16,24},{24,16},{1,9},{9,1},{17,25},{25,17},{2,10},{10... | collective-permute-start | bytes 208904 | tf_op jit(solution)/shard_map/ppermute | solution.py:46
  26.5 13.4 %collective-permute-start.10 = (s16[2,272,128]{2,1,0:T(8,128)(2,1)S(1)}, s16[2,272,128]{2,1,0:T(8,128)(2,1)S(1)}, u32[]{:S(2)}, u32[]{:S(2)}) collective-permute-start(s16[2,272,128]{2,1,0:T(8,128)(2,1)S(1)} %get-tuple-element.46), channel_id=1, source_target_pairs={{0,8},{8,0},{16,24},{24,16},{1,9},{9,1},{17,25},{25,17},{2,10},{10... | collective-permute-start | bytes 417800 | tf_op jit(solution)/shard_map/ppermute | solution.py:46
  32.7 8.3 %collective-permute-start.11 = (s16[2,272,128]{2,1,0:T(8,128)(2,1)S(1)}, s16[2,272,128]{2,1,0:T(8,128)(2,1)S(1)}, u32[]{:S(2)}, u32[]{:S(2)}) collective-permute-start(s16[2,272,128]{2,1,0:T(8,128)(2,1)S(1)} %get-tuple-element.47), channel_id=1, source_target_pairs={{0,16},{8,24},{16,0},{24,8},{1,17},{9,25},{17,1},{25,9},{2,18},{10... | collective-permute-start | bytes 417800 | tf_op jit(solution)/shard_map/ppermute | solution.py:46
  34.8 9.7 %collective-permute-start.12 = (s16[2,272,128]{2,1,0:T(8,128)(2,1)S(1)}, s16[2,272,128]{2,1,0:T(8,128)(2,1)S(1)}, u32[]{:S(2)}, u32[]{:S(2)}) collective-permute-start(s16[2,272,128]{2,1,0:T(8,128)(2,1)S(1)} %get-tuple-element.48), channel_id=1, source_target_pairs={{0,24},{8,16},{16,8},{24,0},{1,25},{9,17},{17,9},{25,1},{2,26},{10... | collective-permute-start | bytes 417800 | tf_op jit(solution)/shard_map/ppermute | solution.py:46
  34.8 10.2 %collective-permute-start.3 = (s16[1,272,128]{2,1,0:T(8,128)(2,1)S(1)}, s16[1,272,128]{2,1,0:T(8,128)(2,1)S(1)}, u32[]{:S(2)}, u32[]{:S(2)}) collective-permute-start(s16[1,272,128]{2,1,0:T(8,128)(2,1)S(1)} %get-tuple-element.39), channel_id=1, source_target_pairs={{0,16},{8,24},{16,0},{24,8},{1,17},{9,25},{17,1},{25,9},{2,18},{10... | collective-permute-start | bytes 208904 | tf_op jit(solution)/shard_map/ppermute | solution.py:46
  38.3 8.7 %collective-permute-start.4 = (s16[1,272,128]{2,1,0:T(8,128)(2,1)S(1)}, s16[1,272,128]{2,1,0:T(8,128)(2,1)S(1)}, u32[]{:S(2)}, u32[]{:S(2)}) collective-permute-start(s16[1,272,128]{2,1,0:T(8,128)(2,1)S(1)} %get-tuple-element.40), channel_id=1, source_target_pairs={{0,24},{8,16},{16,8},{24,0},{1,25},{9,17},{17,9},{25,1},{2,26},{10... | collective-permute-start | bytes 208904 | tf_op jit(solution)/shard_map/ppermute | solution.py:46
  39.9 7.9 %collective-permute-start.17 = (s16[1,272,128]{2,1,0:T(8,128)(2,1)S(1)}, s16[1,272,128]{2,1,0:T(8,128)(2,1)S(1)}, u32[]{:S(2)}, u32[]{:S(2)}) collective-permute-start(s16[1,272,128]{2,1,0:T(8,128)(2,1)S(1)} %get-tuple-element.52), channel_id=1, source_target_pairs={{0,8},{8,0},{16,24},{24,16},{1,9},{9,1},{17,25},{25,17},{2,10},{10... | collective-permute-start | bytes 208904 | tf_op jit(solution)/shard_map/ppermute | solution.py:46
  40.9 6.9 %collective-permute-start.18 = (s16[1,272,128]{2,1,0:T(8,128)(2,1)S(1)}, s16[1,272,128]{2,1,0:T(8,128)(2,1)S(1)}, u32[]{:S(2)}, u32[]{:S(2)}) collective-permute-start(s16[1,272,128]{2,1,0:T(8,128)(2,1)S(1)} %get-tuple-element.53), channel_id=1, source_target_pairs={{0,16},{8,24},{16,0},{24,8},{1,17},{9,25},{17,1},{25,9},{2,18},{10... | collective-permute-start | bytes 208904 | tf_op jit(solution)/shard_map/ppermute | solution.py:46
  44.5 4.3 %collective-permute-start.19 = (s16[1,272,128]{2,1,0:T(8,128)(2,1)S(1)}, s16[1,272,128]{2,1,0:T(8,128)(2,1)S(1)}, u32[]{:S(2)}, u32[]{:S(2)}) collective-permute-start(s16[1,272,128]{2,1,0:T(8,128)(2,1)S(1)} %get-tuple-element.54), channel_id=1, source_target_pairs={{0,24},{8,16},{16,8},{24,0},{1,25},{9,17},{17,9},{25,1},{2,26},{10... | collective-permute-start | bytes 208904 | tf_op jit(solution)/shard_map/ppermute | solution.py:46
  45.1 6.9 %collective-permute-start.13 = (f32[2,128,128]{2,1,0:T(8,128)S(1)}, f32[2,128,128]{2,1,0:T(8,128)S(1)}, u32[]{:S(2)}, u32[]{:S(2)}) collective-permute-start(f32[2,128,128]{2,1,0:T(8,128)S(1)} %get-tuple-element.50), channel_id=1, source_target_pairs={{0,32},{32,0},{1,33},{33,1},{2,34},{34,2},{3,35},{35,3},{4,36},{36... | collective-permute-start | bytes 393224 | tf_op jit(solution)/shard_map/ppermute | solution.py:46
  47.2 4.8 %collective-permute-start.5 = (f32[1,128,128]{2,1,0:T(8,128)S(1)}, f32[1,128,128]{2,1,0:T(8,128)S(1)}, u32[]{:S(2)}, u32[]{:S(2)}) collective-permute-start(f32[1,128,128]{2,1,0:T(8,128)S(1)} %get-tuple-element.42), channel_id=1, source_target_pairs={{0,32},{32,0},{1,33},{33,1},{2,34},{34,2},{3,35},{35,3},{4,36},{36... | collective-permute-start | bytes 196616 | tf_op jit(solution)/shard_map/ppermute | solution.py:46
  48.9 4.4 %collective-permute-start.20 = (f32[1,128,128]{2,1,0:T(8,128)S(1)}, f32[1,128,128]{2,1,0:T(8,128)S(1)}, u32[]{:S(2)}, u32[]{:S(2)}) collective-permute-start(f32[1,128,128]{2,1,0:T(8,128)S(1)} %get-tuple-element.56), channel_id=1, source_target_pairs={{0,32},{32,0},{1,33},{33,1},{2,34},{34,2},{3,35},{35,3},{4,36},{36... | collective-permute-start | bytes 196616 | tf_op jit(solution)/shard_map/ppermute | solution.py:46
  53.5 8.8 %collective-permute-start.21 = (s16[144,128]{1,0:T(8,128)(2,1)S(1)}, s16[144,128]{1,0:T(8,128)(2,1)S(1)}, u32[]{:S(2)}, u32[]{:S(2)}) collective-permute-start(s16[144,128]{1,0:T(8,128)(2,1)S(1)} %get-tuple-element.58), channel_id=1, source_target_pairs={{0,64},{64,0},{128,192},{192,128},{1,65},{65,1},{129,193},{193,129... | collective-permute-start | bytes 110600 | tf_op jit(solution)/shard_map/ppermute | solution.py:46
  56.8 8.0 %collective-permute-start.22 = (s16[144,128]{1,0:T(8,128)(2,1)S(1)}, s16[144,128]{1,0:T(8,128)(2,1)S(1)}, u32[]{:S(2)}, u32[]{:S(2)}) collective-permute-start(s16[144,128]{1,0:T(8,128)(2,1)S(1)} %get-tuple-element.59), channel_id=1, source_target_pairs={{0,128},{64,192},{128,0},{192,64},{1,129},{65,193},{129,1},{193,65... | collective-permute-start | bytes 110600 | tf_op jit(solution)/shard_map/ppermute | solution.py:46
  62.2 6.1 %collective-permute-start.23 = (s16[144,128]{1,0:T(8,128)(2,1)S(1)}, s16[144,128]{1,0:T(8,128)(2,1)S(1)}, u32[]{:S(2)}, u32[]{:S(2)}) collective-permute-start(s16[144,128]{1,0:T(8,128)(2,1)S(1)} %get-tuple-element.60), channel_id=1, source_target_pairs={{0,192},{64,128},{128,64},{192,0},{1,193},{65,129},{129,65},{193,1... | collective-permute-start | bytes 110600 | tf_op jit(solution)/shard_map/ppermute | solution.py:46

commit v3 on v2

--- a/solution.py
+++ b/solution.py
@@ -10,10 +10,10 @@
 
 SBLK = 12
 OCC = 6
-HALF = OCC // 2
 BLOCK = 256
 VS = 128
-ROWS = HALF * 2 * VS
+CUT = 5 * VS
+ROWS = (CUT, 2 * OCC * VS - CUT)
 PARTS = [pl.ds(v, 16) for v in range(0, VS, 16)]
 NX = 4
 NSAMP = 98304
@@ -73,15 +73,15 @@
         for o in range(OCC):
             both = jnp.swapaxes(held[part, o], 0, 1)
             for c in range(2):
-                to = (o % HALF) * 2 * VS + c * VS + part.start
-                (a, b)[o // HALF][to : to + part.size, :] = both[c]
+                to = (2 * o + c) * VS + part.start
+                half, to = (a, to) if to < CUT else (b, to - CUT)
+                half[to : to + part.size, :] = both[c]
 
 
 def relaid(blocks):
-    half = pltpu.VMEM((ROWS, BLOCK), jnp.bfloat16)
     return pl.pallas_call(
         relay_kernel,
-        out_shape=(half,) * 2,
+        out_shape=tuple(pltpu.VMEM((rows, BLOCK), jnp.bfloat16) for rows in ROWS),
         in_specs=[pl.BlockSpec(memory_space=pltpu.HBM)],
         out_specs=(VM,) * 2,
         scratch_shapes=[
@@ -99,17 +99,17 @@
         word = jnp.where((lane == o) & (o < count[0]), ids[o], word)
     word = word.astype(jnp.float32).astype(jnp.bfloat16)
     tags[...] = word
-    for half, out in ((a, tagged_a), (b, tagged_b)):
-        out[:ROWS] = half[...]
-        out[ROWS:] = word
+    for half, out, rows in ((a, tagged_a, ROWS[0]), (b, tagged_b, ROWS[1])):
+        out[:rows] = half[...]
+        out[rows:] = word
 
 
 def tagged(ids, count, halves):
-    more = pltpu.VMEM((ROWS + 16, BLOCK), jnp.bfloat16)
+    more = (pltpu.VMEM((rows + 16, BLOCK), jnp.bfloat16) for rows in ROWS)
     smem = pl.BlockSpec(memory_space=pltpu.SMEM)
     return pl.pallas_call(
         tag_kernel,
-        out_shape=(more, more, pltpu.VMEM((16, BLOCK), jnp.bfloat16)),
+        out_shape=(*more, pltpu.VMEM((16, BLOCK), jnp.bfloat16)),
         in_specs=[smem, smem, VM, VM],
         out_specs=(VM,) * 3,
         cost_estimate=pl.CostEstimate(flops=2 * 256**3, transcendentals=0, bytes_accessed=0),
@@ -126,6 +126,14 @@
         weight = jnp.where(lane == o, float(16**o), weight)
     word = jnp.sum(tags * weight).astype(jnp.int32)
     return [(word >> (4 * o)) & 15 for o in range(OCC)]
+
+
+def slot_of_halves(a, b, o):
+    parts = [
+        a[r : r + VS, :] if r < CUT else b[r - CUT : r - CUT + VS, :]
+        for r in (2 * o * VS, (2 * o + 1) * VS)
+    ]
+    return jnp.concatenate(parts, axis=0)
 
 
 def table_kernel(n, gathers, *refs):
@@ -140,7 +148,7 @@
         cols, refs = refs[0], refs[1:]
         for s, halves in enumerate(((a0, b0), (a1, b1))):
             for o in range(OCC):
-                cols[s, o] = halves[o // HALF][pl.ds((o % HALF) * 256, 256), :]
+                cols[s, o] = slot_of_halves(*halves, o)
     slot_of, acc = refs
     x, core = lax.axis_index("x"), lax.axis_index("vrow")
     for s, ref in enumerate(col_tags):
@@ -157,7 +165,7 @@
             total = None
             for o in range(OCC):
                 slot = slot_of[s, row_ids[j][o]]
-                m = rows[2 * j + o // HALF][pl.ds((o % HALF) * 256, 256), :]
+                m = slot_of_halves(*rows[2 * j : 2 * j + 2], o)
                 m = jnp.where(slot >= 0, m, jnp.zeros_like(m))
                 d = lax.dot_general(
                     m,

time: 70.4 us -> 74.5 us (1.058)
  the two profiles are of different devices: /device:TPU:2 before, /device:TPU:24 now
where the time goes in v3:
time: 74.5 us; the launch traced here: 74.4 us
  starting transfers between devices  36.9 us (50%)
  waiting for transfers between devices  29.2 us (39%)
  Pallas kernels  6.91 us (9%)
  between operations  0.77 us (1%)
    ppermute x24, starting transfers between devices, rotate(): return lax.ppermute(array, axis, [(i, i ^ shift) for i in range(n)])  36.9 us
    ppermute x24, waiting for transfers between devices, rotate(): return lax.ppermute(array, axis, [(i, i ^ shift) for i in range(n)])  29.2 us
    pallas_call x8, Pallas kernels, on_chip(): pl.pallas_call(f, out_shape=out_shape, in_specs=[VM] * len(arrays), out_s...  4.97 us
  transfers between devices with their start and end apart: 24, of which 11 were waited for; matrix products, arithmetic and copies ran while one was open for 0% of the time, Pallas kernels for 6%

profile of v3, /device:TPU:24, one launch (start us, length us, event | category | flops | bytes accessed | tf_op | source)
XLA Modules:
  0.0 74.4 jit_solution(309167299115895695)
XLA Ops:
  0.0 1.3 %shard_map.37 = (bf16[640,256]{1,0:T(8,128)(2,1)S(1)}, bf16[896,256]{1,0:T(8,128)(2,1)S(1)}) custom-call(bf16[128,6,2,256]{3,2,1,0:T(2,128)(2,1)} %blocks.1), custom_call_target="tpu_custom_call" | custom-call | tf_op jit(solution)/shard_map/pallas_call | solution.py:82
  1.4 2.0 %collective-permute-start.9 = (bf16[896,256]{1,0:T(8,128)(2,1)S(1)}, bf16[896,256]{1,0:T(8,128)(2,1)S(1)}, u32[]{:S(2)}, u32[]{:S(2)}) collective-permute-start(bf16[896,256]{1,0:T(8,128)(2,1)S(1)} %get-tuple-element.34.b.refs_4_), channel_id=1, source_target_pairs={{0,3},{1,2},{2,1},{3,0},{4,7},{5,6},{6,5},{7,4},{8,11},{9,10},{10,... | collective-permute-start | bytes 1376264 | tf_op jit(solution)/shard_map/ppermute | solution.py:46
  4.0 0.0 copy-start
  4.0 0.6 copy-done
  4.7 0.6 shard_map.38
  5.3 0.6 collective-permute-start
  5.9 2.0 %collective-permute-start.6 = (bf16[912,256]{1,0:T(8,128)(2,1)S(1)}, bf16[912,256]{1,0:T(8,128)(2,1)S(1)}, u32[]{:S(2)}, u32[]{:S(2)}) collective-permute-start(bf16[912,256]{1,0:T(8,128)(2,1)S(1)} %get-tuple-element.36), channel_id=1, source_target_pairs={{0,1},{1,0},{2,3},{3,2},{4,5},{5,4},{6,7},{7,6},{8,9},{9,8},{10,11... | collective-permute-start | bytes 1400840 | tf_op jit(solution)/shard_map/ppermute | solution.py:46
  7.9 0.0 collective-permute-done.1.refs_5_
  7.9 1.3 %collective-permute-start.7 = (bf16[656,256]{1,0:T(8,128)(2,1)S(1)}, bf16[656,256]{1,0:T(8,128)(2,1)S(1)}, u32[]{:S(2)}, u32[]{:S(2)}) collective-permute-start(bf16[656,256]{1,0:T(8,128)(2,1)S(1)} %get-tuple-element.43), channel_id=1, source_target_pairs={{0,3},{1,2},{2,1},{3,0},{4,7},{5,6},{6,5},{7,4},{8,11},{9,10},{10,... | collective-permute-start | bytes 1007624 | tf_op jit(solution)/shard_map/ppermute | solution.py:46
  9.2 6.8 %collective-permute-done.9.refs_8_ = bf16[896,256]{1,0:T(8,128)(2,1)S(1)} collective-permute-done((bf16[896,256]{1,0:T(8,128)(2,1)S(1)}, bf16[896,256]{1,0:T(8,128)(2,1)S(1)}, u32[]{:S(2)}, u32[]{:S(2)}) %collective-permute-start.9) | collective-permute-done | bytes 458784 | tf_op jit(solution)/shard_map/ppermute | solution.py:46
  16.0 0.0 collective-permute-start.16
  16.0 0.4 collective-permute-done.8.refs_5_
  16.5 1.4 %collective-permute-start.15 = (bf16[640,256]{1,0:T(8,128)(2,1)S(1)}, bf16[640,256]{1,0:T(8,128)(2,1)S(1)}, u32[]{:S(2)}, u32[]{:S(2)}) collective-permute-start(bf16[640,256]{1,0:T(8,128)(2,1)S(1)} %collective-permute-done.8.refs_5_), channel_id=1, source_target_pairs={{0,3},{1,2},{2,1},{3,0},{4,7},{5,6},{6,5},{7,4},{8,11},{9,10},{10,... | collective-permute-start | bytes 983048 | tf_op jit(solution)/shard_map/ppermute | solution.py:46
  17.8 2.3 %collective-permute-start.14 = (bf16[16,256]{1,0:T(8,128)(2,1)S(1)}, bf16[16,256]{1,0:T(8,128)(2,1)S(1)}, u32[]{:S(2)}, u32[]{:S(2)}) collective-permute-start(bf16[16,256]{1,0:T(8,128)(2,1)S(1)} %get-tuple-element.35.refs_0_.refs_2_), channel_id=1, source_target_pairs={{0,2},{1,3},{2,0},{3,1},{4,6},{5,7},{6,4},{7,5},{8,10},{9,11},{10,... | collective-permute-start | bytes 24584 | tf_op jit(solution)/shard_map/ppermute | solution.py:46
  20.1 1.0 %shard_map.39 = (f32[1,256,128]{2,1,0:T(8,128)S(1)}, s16[1,272,128]{2,1,0:T(8,128)(2,1)S(1)}, s16[1,272,128]{2,1,0:T(8,128)(2,1)S(1)}, s16[1,272,128]{2,1,0:T(8,128)(2,1)S(1)}, bf16[2,6,256,256]{3,2,1,0:T(8,128)(2,1)S(1)}) custom-call(bf16[16,256]{1,0:T(8,128)(2,1)S(1)} %get-tuple-element.35.refs_0_.refs_2_, ...), custom_call_target="tpu_custom_call" | custom-call | flops 402653184 | tf_op jit(solution)/shard_map/pallas_call | solution.py:32
  21.2 2.1 %collective-permute-done.7.refs_3_.refs_7_ = bf16[656,256]{1,0:T(8,128)(2,1)S(1)} collective-permute-done((bf16[656,256]{1,0:T(8,128)(2,1)S(1)}, bf16[656,256]{1,0:T(8,128)(2,1)S(1)}, u32[]{:S(2)}, u32[]{:S(2)}) %collective-permute-start.7) | collective-permute-done | bytes 335904 | tf_op jit(solution)/shard_map/ppermute | solution.py:46
  23.2 1.5 %collective-permute-start.2 = (s16[1,272,128]{2,1,0:T(8,128)(2,1)S(1)}, s16[1,272,128]{2,1,0:T(8,128)(2,1)S(1)}, u32[]{:S(2)}, u32[]{:S(2)}) collective-permute-start(s16[1,272,128]{2,1,0:T(8,128)(2,1)S(1)} %get-tuple-element.38), channel_id=1, source_target_pairs={{0,8},{8,0},{16,24},{24,16},{1,9},{9,1},{17,25},{25,17},{2,10},{10... | collective-permute-start | bytes 208904 | tf_op jit(solution)/shard_map/ppermute | solution.py:46
  24.7 1.7 %collective-permute-done.6.refs_2_.refs_6_ = bf16[912,256]{1,0:T(8,128)(2,1)S(1)} collective-permute-done((bf16[912,256]{1,0:T(8,128)(2,1)S(1)}, bf16[912,256]{1,0:T(8,128)(2,1)S(1)}, u32[]{:S(2)}, u32[]{:S(2)}) %collective-permute-start.6) | collective-permute-done | bytes 466976 | tf_op jit(solution)/shard_map/ppermute | solution.py:46
  26.5 1.5 %shard_map.41 = (f32[2,256,128]{2,1,0:T(8,128)S(1)}, s16[2,272,128]{2,1,0:T(8,128)(2,1)S(1)}, s16[2,272,128]{2,1,0:T(8,128)(2,1)S(1)}, s16[2,272,128]{2,1,0:T(8,128)(2,1)S(1)}) custom-call(bf16[16,256]{1,0:T(8,128)(2,1)S(1)} %get-tuple-element.35.refs_0_.refs_2_, bf16[912,256]{1,0:T(8,128)(2,1)S(1)} %collective-permute-done.refs_1_.refs_6_, ...), custom_call_target="tpu_custom_call" | custom-call | flops 805306368 | tf_op jit(solution)/shard_map/pallas_call | solution.py:32
  28.0 0.1 collective-permute-start.10
  28.1 8.2 %collective-permute-done.14.refs_2_ = bf16[16,256]{1,0:T(8,128)(2,1)S(1)} collective-permute-done((bf16[16,256]{1,0:T(8,128)(2,1)S(1)}, bf16[16,256]{1,0:T(8,128)(2,1)S(1)}, u32[]{:S(2)}, u32[]{:S(2)}) %collective-permute-start.14) | collective-permute-done | bytes 8224 | tf_op jit(solution)/shard_map/ppermute | solution.py:46
  36.4 3.0 %collective-permute-start.11 = (s16[2,272,128]{2,1,0:T(8,128)(2,1)S(1)}, s16[2,272,128]{2,1,0:T(8,128)(2,1)S(1)}, u32[]{:S(2)}, u32[]{:S(2)}) collective-permute-start(s16[2,272,128]{2,1,0:T(8,128)(2,1)S(1)} %get-tuple-element.47), channel_id=1, source_target_pairs={{0,16},{8,24},{16,0},{24,8},{1,17},{9,25},{17,1},{25,9},{2,18},{10... | collective-permute-start | bytes 417800 | tf_op jit(solution)/shard_map/ppermute | solution.py:46
  39.4 1.1 %collective-permute-start.12 = (s16[2,272,128]{2,1,0:T(8,128)(2,1)S(1)}, s16[2,272,128]{2,1,0:T(8,128)(2,1)S(1)}, u32[]{:S(2)}, u32[]{:S(2)}) collective-permute-start(s16[2,272,128]{2,1,0:T(8,128)(2,1)S(1)} %get-tuple-element.48), channel_id=1, source_target_pairs={{0,24},{8,16},{16,8},{24,0},{1,25},{9,17},{17,9},{25,1},{2,26},{10... | collective-permute-start | bytes 417800 | tf_op jit(solution)/shard_map/ppermute | solution.py:46
  40.5 0.0 collective-permute-done.15.refs_4_
  40.5 1.5 %collective-permute-start.3 = (s16[1,272,128]{2,1,0:T(8,128)(2,1)S(1)}, s16[1,272,128]{2,1,0:T(8,128)(2,1)S(1)}, u32[]{:S(2)}, u32[]{:S(2)}) collective-permute-start(s16[1,272,128]{2,1,0:T(8,128)(2,1)S(1)} %get-tuple-element.39), channel_id=1, source_target_pairs={{0,16},{8,24},{16,0},{24,8},{1,17},{9,25},{17,1},{25,9},{2,18},{10... | collective-permute-start | bytes 208904 | tf_op jit(solution)/shard_map/ppermute | solution.py:46
  42.0 0.0 collective-permute-done.16.refs_5_
  42.0 0.7 collective-permute-start.4
  42.7 1.0 %shard_map.43 = (f32[1,256,128]{2,1,0:T(8,128)S(1)}, s16[1,272,128]{2,1,0:T(8,128)(2,1)S(1)}, s16[1,272,128]{2,1,0:T(8,128)(2,1)S(1)}, s16[1,272,128]{2,1,0:T(8,128)(2,1)S(1)}) custom-call(bf16[16,256]{1,0:T(8,128)(2,1)S(1)} %get-tuple-element.35.refs_0_.refs_2_, bf16[912,256]{1,0:T(8,128)(2,1)S(1)} %collective-permute-done.refs_1_.refs_6_, ...), custom_call_target="tpu_custom_call" | custom-call | flops 402653184 | tf_op jit(solution)/shard_map/pallas_call | solution.py:32
  43.8 1.4 %collective-permute-start.17 = (s16[1,272,128]{2,1,0:T(8,128)(2,1)S(1)}, s16[1,272,128]{2,1,0:T(8,128)(2,1)S(1)}, u32[]{:S(2)}, u32[]{:S(2)}) collective-permute-start(s16[1,272,128]{2,1,0:T(8,128)(2,1)S(1)} %get-tuple-element.52), channel_id=1, source_target_pairs={{0,8},{8,0},{16,24},{24,16},{1,9},{9,1},{17,25},{25,17},{2,10},{10... | collective-permute-start | bytes 208904 | tf_op jit(solution)/shard_map/ppermute | solution.py:46
  45.1 2.7 %collective-permute-start.18 = (s16[1,272,128]{2,1,0:T(8,128)(2,1)S(1)}, s16[1,272,128]{2,1,0:T(8,128)(2,1)S(1)}, u32[]{:S(2)}, u32[]{:S(2)}) collective-permute-start(s16[1,272,128]{2,1,0:T(8,128)(2,1)S(1)} %get-tuple-element.53), channel_id=1, source_target_pairs={{0,16},{8,24},{16,0},{24,8},{1,17},{9,25},{17,1},{25,9},{2,18},{10... | collective-permute-start | bytes 208904 | tf_op jit(solution)/shard_map/ppermute | solution.py:46
  47.9 0.8 %collective-permute-done.12.refs_3_ = s16[2,272,128]{2,1,0:T(8,128)(2,1)S(1)} collective-permute-done((s16[2,272,128]{2,1,0:T(8,128)(2,1)S(1)}, s16[2,272,128]{2,1,0:T(8,128)(2,1)S(1)}, u32[]{:S(2)}, u32[]{:S(2)}) %collective-permute-start.12) | collective-permute-done | bytes 139296 | tf_op jit(solution)/shard_map/ppermute | solution.py:46
  48.6 2.3 %collective-permute-start.19 = (s16[1,272,128]{2,1,0:T(8,128)(2,1)S(1)}, s16[1,272,128]{2,1,0:T(8,128)(2,1)S(1)}, u32[]{:S(2)}, u32[]{:S(2)}) collective-permute-start(s16[1,272,128]{2,1,0:T(8,128)(2,1)S(1)} %get-tuple-element.54), channel_id=1, source_target_pairs={{0,24},{8,16},{16,8},{24,0},{1,25},{9,17},{17,9},{25,1},{2,26},{10... | collective-permute-start | bytes 208904 | tf_op jit(solution)/shard_map/ppermute | solution.py:46
  50.9 0.2 shard_map.42
  51.1 0.0 collective-permute-done.3.refs_2_
  51.1 2.0 %collective-permute-start.13 = (f32[2,128,128]{2,1,0:T(8,128)S(1)}, f32[2,128,128]{2,1,0:T(8,128)S(1)}, u32[]{:S(2)}, u32[]{:S(2)}) collective-permute-start(f32[2,128,128]{2,1,0:T(8,128)S(1)} %get-tuple-element.50), channel_id=1, source_target_pairs={{0,32},{32,0},{1,33},{33,1},{2,34},{34,2},{3,35},{35,3},{4,36},{36... | collective-permute-start | bytes 393224 | tf_op jit(solution)/shard_map/ppermute | solution.py:46
  53.1 0.1 shard_map.40
  53.2 0.2 collective-permute-start.5
  53.5 0.7 collective-permute-done.19.refs_3_
  54.1 0.1 shard_map.44
  54.3 2.0 %collective-permute-start.20 = (f32[1,128,128]{2,1,0:T(8,128)S(1)}, f32[1,128,128]{2,1,0:T(8,128)S(1)}, u32[]{:S(2)}, u32[]{:S(2)}) collective-permute-start(f32[1,128,128]{2,1,0:T(8,128)S(1)} %get-tuple-element.56), channel_id=1, source_target_pairs={{0,32},{32,0},{1,33},{33,1},{2,34},{34,2},{3,35},{35,3},{4,36},{36... | collective-permute-start | bytes 196616 | tf_op jit(solution)/shard_map/ppermute | solution.py:46
  56.3 1.7 %collective-permute-done.5.refs_1_ = f32[1,128,128]{2,1,0:T(8,128)S(1)} collective-permute-done((f32[1,128,128]{2,1,0:T(8,128)S(1)}, f32[1,128,128]{2,1,0:T(8,128)S(1)}, u32[]{:S(2)}, u32[]{:S(2)}) %collective-permute-start.5) | collective-permute-done | bytes 65568 | tf_op jit(solution)/shard_map/ppermute | solution.py:46
  57.9 0.7 collective-permute-done.20.refs_5_
  58.6 0.2 shard_map.45
  58.9 3.4 %collective-permute-start.21 = (s16[144,128]{1,0:T(8,128)(2,1)S(1)}, s16[144,128]{1,0:T(8,128)(2,1)S(1)}, u32[]{:S(2)}, u32[]{:S(2)}) collective-permute-start(s16[144,128]{1,0:T(8,128)(2,1)S(1)} %get-tuple-element.58), channel_id=1, source_target_pairs={{0,64},{64,0},{128,192},{192,128},{1,65},{65,1},{129,193},{193,129... | collective-permute-start | bytes 110600 | tf_op jit(solution)/shard_map/ppermute | solution.py:46
  62.2 5.4 %collective-permute-start.22 = (s16[144,128]{1,0:T(8,128)(2,1)S(1)}, s16[144,128]{1,0:T(8,128)(2,1)S(1)}, u32[]{:S(2)}, u32[]{:S(2)}) collective-permute-start(s16[144,128]{1,0:T(8,128)(2,1)S(1)} %get-tuple-element.59), channel_id=1, source_target_pairs={{0,128},{64,192},{128,0},{192,64},{1,129},{65,193},{129,1},{193,65... | collective-permute-start | bytes 110600 | tf_op jit(solution)/shard_map/ppermute | solution.py:46
  67.6 3.2 %collective-permute-done.22.refs_2_ = s16[144,128]{1,0:T(8,128)(2,1)S(1)} collective-permute-done((s16[144,128]{1,0:T(8,128)(2,1)S(1)}, s16[144,128]{1,0:T(8,128)(2,1)S(1)}, u32[]{:S(2)}, u32[]{:S(2)}) %collective-permute-start.22) | collective-permute-done | bytes 36896 | tf_op jit(solution)/shard_map/ppermute | solution.py:46
  70.9 2.8 %collective-permute-done.23.refs_3_ = s16[144,128]{1,0:T(8,128)(2,1)S(1)} collective-permute-done((s16[144,128]{1,0:T(8,128)(2,1)S(1)}, s16[144,128]{1,0:T(8,128)(2,1)S(1)}, u32[]{:S(2)}, u32[]{:S(2)}) %collective-permute-start.23) | collective-permute-done | bytes 36896 | tf_op jit(solution)/shard_map/ppermute | solution.py:46
  73.7 0.7 shard_map.46
  (12 shorter events, 0.0 us)
Async XLA Ops:
  1.4 14.7 %collective-permute-start.9 = (bf16[896,256]{1,0:T(8,128)(2,1)S(1)}, bf16[896,256]{1,0:T(8,128)(2,1)S(1)}, u32[]{:S(2)}, u32[]{:S(2)}) collective-permute-start(bf16[896,256]{1,0:T(8,128)(2,1)S(1)} %get-tuple-element.34.b.refs_4_), channel_id=1, source_target_pairs={{0,3},{1,2},{2,1},{3,0},{4,7},{5,6},{6,5},{7,4},{8,11},{9,10},{10,... | collective-permute-start | bytes 1376264 | tf_op jit(solution)/shard_map/ppermute | solution.py:46
  3.4 4.5 %collective-permute-start.1 = (bf16[640,256]{1,0:T(8,128)(2,1)S(1)}, bf16[640,256]{1,0:T(8,128)(2,1)S(1)}, u32[]{:S(2)}, u32[]{:S(2)}) collective-permute-start(bf16[640,256]{1,0:T(8,128)(2,1)S(1)} %get-tuple-element.33.a.refs_3_), channel_id=1, source_target_pairs={{0,4},{4,0},{1,5},{5,1},{2,6},{6,2},{3,7},{7,3},{8,12},{12,8},{9,1... | collective-permute-start | bytes 983048 | tf_op jit(solution)/shard_map/ppermute | solution.py:46
  4.0 0.7 copy-start
  5.3 12.6 %collective-permute-start = (bf16[912,256]{1,0:T(8,128)(2,1)S(1)}, bf16[912,256]{1,0:T(8,128)(2,1)S(1)}, u32[]{:S(2)}, u32[]{:S(2)}) collective-permute-start(bf16[912,256]{1,0:T(8,128)(2,1)S(1)} %get-tuple-element.36), channel_id=1, source_target_pairs={{0,4},{4,0},{1,5},{5,1},{2,6},{6,2},{3,7},{7,3},{8,12},{12,8},{9,1... | collective-permute-start | bytes 1400840 | tf_op jit(solution)/shard_map/ppermute | solution.py:46
  5.9 10.6 %collective-permute-start.8 = (bf16[640,256]{1,0:T(8,128)(2,1)S(1)}, bf16[640,256]{1,0:T(8,128)(2,1)S(1)}, u32[]{:S(2)}, u32[]{:S(2)}) collective-permute-start(bf16[640,256]{1,0:T(8,128)(2,1)S(1)} %get-tuple-element.33.a.refs_3_), channel_id=1, source_target_pairs={{0,1},{1,0},{2,3},{3,2},{4,5},{5,4},{6,7},{7,6},{8,9},{9,8},{10,11... | collective-permute-start | bytes 983048 | tf_op jit(solution)/shard_map/ppermute | solution.py:46
  5.9 20.6 %collective-permute-start.6 = (bf16[912,256]{1,0:T(8,128)(2,1)S(1)}, bf16[912,256]{1,0:T(8,128)(2,1)S(1)}, u32[]{:S(2)}, u32[]{:S(2)}) collective-permute-start(bf16[912,256]{1,0:T(8,128)(2,1)S(1)} %get-tuple-element.36), channel_id=1, source_target_pairs={{0,1},{1,0},{2,3},{3,2},{4,5},{5,4},{6,7},{7,6},{8,9},{9,8},{10,11... | collective-permute-start | bytes 1400840 | tf_op jit(solution)/shard_map/ppermute | solution.py:46
  7.9 15.3 %collective-permute-start.7 = (bf16[656,256]{1,0:T(8,128)(2,1)S(1)}, bf16[656,256]{1,0:T(8,128)(2,1)S(1)}, u32[]{:S(2)}, u32[]{:S(2)}) collective-permute-start(bf16[656,256]{1,0:T(8,128)(2,1)S(1)} %get-tuple-element.43), channel_id=1, source_target_pairs={{0,3},{1,2},{2,1},{3,0},{4,7},{5,6},{6,5},{7,4},{8,11},{9,10},{10,... | collective-permute-start | bytes 1007624 | tf_op jit(solution)/shard_map/ppermute | solution.py:46
  16.0 26.0 %collective-permute-start.16 = (bf16[896,256]{1,0:T(8,128)(2,1)S(1)}, bf16[896,256]{1,0:T(8,128)(2,1)S(1)}, u32[]{:S(2)}, u32[]{:S(2)}) collective-permute-start(bf16[896,256]{1,0:T(8,128)(2,1)S(1)} %collective-permute-done.9.refs_8_), channel_id=1, source_target_pairs={{0,1},{1,0},{2,3},{3,2},{4,5},{5,4},{6,7},{7,6},{8,9},{9,8},{10,11... | collective-permute-start | bytes 1376264 | tf_op jit(solution)/shard_map/ppermute | solution.py:46
  16.5 24.1 %collective-permute-start.15 = (bf16[640,256]{1,0:T(8,128)(2,1)S(1)}, bf16[640,256]{1,0:T(8,128)(2,1)S(1)}, u32[]{:S(2)}, u32[]{:S(2)}) collective-permute-start(bf16[640,256]{1,0:T(8,128)(2,1)S(1)} %collective-permute-done.8.refs_5_), channel_id=1, source_target_pairs={{0,3},{1,2},{2,1},{3,0},{4,7},{5,6},{6,5},{7,4},{8,11},{9,10},{10,... | collective-permute-start | bytes 983048 | tf_op jit(solution)/shard_map/ppermute | solution.py:46
  17.8 18.5 %collective-permute-start.14 = (bf16[16,256]{1,0:T(8,128)(2,1)S(1)}, bf16[16,256]{1,0:T(8,128)(2,1)S(1)}, u32[]{:S(2)}, u32[]{:S(2)}) collective-permute-start(bf16[16,256]{1,0:T(8,128)(2,1)S(1)} %get-tuple-element.35.refs_0_.refs_2_), channel_id=1, source_target_pairs={{0,2},{1,3},{2,0},{3,1},{4,6},{5,7},{6,4},{7,5},{8,10},{9,11},{10,... | collective-permute-start | bytes 24584 | tf_op jit(solution)/shard_map/ppermute | solution.py:46
  23.2 16.1 %collective-permute-start.2 = (s16[1,272,128]{2,1,0:T(8,128)(2,1)S(1)}, s16[1,272,128]{2,1,0:T(8,128)(2,1)S(1)}, u32[]{:S(2)}, u32[]{:S(2)}) collective-permute-start(s16[1,272,128]{2,1,0:T(8,128)(2,1)S(1)} %get-tuple-element.38), channel_id=1, source_target_pairs={{0,8},{8,0},{16,24},{24,16},{1,9},{9,1},{17,25},{25,17},{2,10},{10... | collective-permute-start | bytes 208904 | tf_op jit(solution)/shard_map/ppermute | solution.py:46
  28.0 15.8 %collective-permute-start.10 = (s16[2,272,128]{2,1,0:T(8,128)(2,1)S(1)}, s16[2,272,128]{2,1,0:T(8,128)(2,1)S(1)}, u32[]{:S(2)}, u32[]{:S(2)}) collective-permute-start(s16[2,272,128]{2,1,0:T(8,128)(2,1)S(1)} %get-tuple-element.46), channel_id=1, source_target_pairs={{0,8},{8,0},{16,24},{24,16},{1,9},{9,1},{17,25},{25,17},{2,10},{10... | collective-permute-start | bytes 417800 | tf_op jit(solution)/shard_map/ppermute | solution.py:46
  36.4 8.8 %collective-permute-start.11 = (s16[2,272,128]{2,1,0:T(8,128)(2,1)S(1)}, s16[2,272,128]{2,1,0:T(8,128)(2,1)S(1)}, u32[]{:S(2)}, u32[]{:S(2)}) collective-permute-start(s16[2,272,128]{2,1,0:T(8,128)(2,1)S(1)} %get-tuple-element.47), channel_id=1, source_target_pairs={{0,16},{8,24},{16,0},{24,8},{1,17},{9,25},{17,1},{25,9},{2,18},{10... | collective-permute-start | bytes 417800 | tf_op jit(solution)/shard_map/ppermute | solution.py:46
  39.4 9.2 %collective-permute-start.12 = (s16[2,272,128]{2,1,0:T(8,128)(2,1)S(1)}, s16[2,272,128]{2,1,0:T(8,128)(2,1)S(1)}, u32[]{:S(2)}, u32[]{:S(2)}) collective-permute-start(s16[2,272,128]{2,1,0:T(8,128)(2,1)S(1)} %get-tuple-element.48), channel_id=1, source_target_pairs={{0,24},{8,16},{16,8},{24,0},{1,25},{9,17},{17,9},{25,1},{2,26},{10... | collective-permute-start | bytes 417800 | tf_op jit(solution)/shard_map/ppermute | solution.py:46
  40.5 10.6 %collective-permute-start.3 = (s16[1,272,128]{2,1,0:T(8,128)(2,1)S(1)}, s16[1,272,128]{2,1,0:T(8,128)(2,1)S(1)}, u32[]{:S(2)}, u32[]{:S(2)}) collective-permute-start(s16[1,272,128]{2,1,0:T(8,128)(2,1)S(1)} %get-tuple-element.39), channel_id=1, source_target_pairs={{0,16},{8,24},{16,0},{24,8},{1,17},{9,25},{17,1},{25,9},{2,18},{10... | collective-permute-start | bytes 208904 | tf_op jit(solution)/shard_map/ppermute | solution.py:46
  42.0 11.1 %collective-permute-start.4 = (s16[1,272,128]{2,1,0:T(8,128)(2,1)S(1)}, s16[1,272,128]{2,1,0:T(8,128)(2,1)S(1)}, u32[]{:S(2)}, u32[]{:S(2)}) collective-permute-start(s16[1,272,128]{2,1,0:T(8,128)(2,1)S(1)} %get-tuple-element.40), channel_id=1, source_target_pairs={{0,24},{8,16},{16,8},{24,0},{1,25},{9,17},{17,9},{25,1},{2,26},{10... | collective-permute-start | bytes 208904 | tf_op jit(solution)/shard_map/ppermute | solution.py:46
  43.8 9.7 %collective-permute-start.17 = (s16[1,272,128]{2,1,0:T(8,128)(2,1)S(1)}, s16[1,272,128]{2,1,0:T(8,128)(2,1)S(1)}, u32[]{:S(2)}, u32[]{:S(2)}) collective-permute-start(s16[1,272,128]{2,1,0:T(8,128)(2,1)S(1)} %get-tuple-element.52), channel_id=1, source_target_pairs={{0,8},{8,0},{16,24},{24,16},{1,9},{9,1},{17,25},{25,17},{2,10},{10... | collective-permute-start | bytes 208904 | tf_op jit(solution)/shard_map/ppermute | solution.py:46
  45.1 8.3 %collective-permute-start.18 = (s16[1,272,128]{2,1,0:T(8,128)(2,1)S(1)}, s16[1,272,128]{2,1,0:T(8,128)(2,1)S(1)}, u32[]{:S(2)}, u32[]{:S(2)}) collective-permute-start(s16[1,272,128]{2,1,0:T(8,128)(2,1)S(1)} %get-tuple-element.53), channel_id=1, source_target_pairs={{0,16},{8,24},{16,0},{24,8},{1,17},{9,25},{17,1},{25,9},{2,18},{10... | collective-permute-start | bytes 208904 | tf_op jit(solution)/shard_map/ppermute | solution.py:46
  48.6 5.5 %collective-permute-start.19 = (s16[1,272,128]{2,1,0:T(8,128)(2,1)S(1)}, s16[1,272,128]{2,1,0:T(8,128)(2,1)S(1)}, u32[]{:S(2)}, u32[]{:S(2)}) collective-permute-start(s16[1,272,128]{2,1,0:T(8,128)(2,1)S(1)} %get-tuple-element.54), channel_id=1, source_target_pairs={{0,24},{8,16},{16,8},{24,0},{1,25},{9,17},{17,9},{25,1},{2,26},{10... | collective-permute-start | bytes 208904 | tf_op jit(solution)/shard_map/ppermute | solution.py:46
  51.1 6.8 %collective-permute-start.13 = (f32[2,128,128]{2,1,0:T(8,128)S(1)}, f32[2,128,128]{2,1,0:T(8,128)S(1)}, u32[]{:S(2)}, u32[]{:S(2)}) collective-permute-start(f32[2,128,128]{2,1,0:T(8,128)S(1)} %get-tuple-element.50), channel_id=1, source_target_pairs={{0,32},{32,0},{1,33},{33,1},{2,34},{34,2},{3,35},{35,3},{4,36},{36... | collective-permute-start | bytes 393224 | tf_op jit(solution)/shard_map/ppermute | solution.py:46
  53.2 4.7 %collective-permute-start.5 = (f32[1,128,128]{2,1,0:T(8,128)S(1)}, f32[1,128,128]{2,1,0:T(8,128)S(1)}, u32[]{:S(2)}, u32[]{:S(2)}) collective-permute-start(f32[1,128,128]{2,1,0:T(8,128)S(1)} %get-tuple-element.42), channel_id=1, source_target_pairs={{0,32},{32,0},{1,33},{33,1},{2,34},{34,2},{3,35},{35,3},{4,36},{36... | collective-permute-start | bytes 196616 | tf_op jit(solution)/shard_map/ppermute | solution.py:46
  54.3 4.4 %collective-permute-start.20 = (f32[1,128,128]{2,1,0:T(8,128)S(1)}, f32[1,128,128]{2,1,0:T(8,128)S(1)}, u32[]{:S(2)}, u32[]{:S(2)}) collective-permute-start(f32[1,128,128]{2,1,0:T(8,128)S(1)} %get-tuple-element.56), channel_id=1, source_target_pairs={{0,32},{32,0},{1,33},{33,1},{2,34},{34,2},{3,35},{35,3},{4,36},{36... | collective-permute-start | bytes 196616 | tf_op jit(solution)/shard_map/ppermute | solution.py:46
  58.9 8.7 %collective-permute-start.21 = (s16[144,128]{1,0:T(8,128)(2,1)S(1)}, s16[144,128]{1,0:T(8,128)(2,1)S(1)}, u32[]{:S(2)}, u32[]{:S(2)}) collective-permute-start(s16[144,128]{1,0:T(8,128)(2,1)S(1)} %get-tuple-element.58), channel_id=1, source_target_pairs={{0,64},{64,0},{128,192},{192,128},{1,65},{65,1},{129,193},{193,129... | collective-permute-start | bytes 110600 | tf_op jit(solution)/shard_map/ppermute | solution.py:46
  62.2 8.6 %collective-permute-start.22 = (s16[144,128]{1,0:T(8,128)(2,1)S(1)}, s16[144,128]{1,0:T(8,128)(2,1)S(1)}, u32[]{:S(2)}, u32[]{:S(2)}) collective-permute-start(s16[144,128]{1,0:T(8,128)(2,1)S(1)} %get-tuple-element.59), channel_id=1, source_target_pairs={{0,128},{64,192},{128,0},{192,64},{1,129},{65,193},{129,1},{193,65... | collective-permute-start | bytes 110600 | tf_op jit(solution)/shard_map/ppermute | solution.py:46
  67.6 6.1 %collective-permute-start.23 = (s16[144,128]{1,0:T(8,128)(2,1)S(1)}, s16[144,128]{1,0:T(8,128)(2,1)S(1)}, u32[]{:S(2)}, u32[]{:S(2)}) collective-permute-start(s16[144,128]{1,0:T(8,128)(2,1)S(1)} %get-tuple-element.60), channel_id=1, source_target_pairs={{0,192},{64,128},{128,64},{192,0},{1,193},{65,129},{129,65},{193,1... | collective-permute-start | bytes 110600 | tf_op jit(solution)/shard_map/ppermute | solution.py:46
